TPU v7x, 256 devices: a whole 4x4x8 slice. The times are simulated.
256 devices in a mesh: obs: 64 (over z, y, core), rep: 4 (over x).
Axes of the slice: x: 4, y: 4, z: 8, core: 2. Of those that a mesh axis runs over, the one named last changes fastest.
Arguments:
- jacobians: float32 [18, 8388608], P(None, ('obs', 'rep')), may hold values from -3 to 3
- residuals: float32 [2, 8388608], P(None, ('obs', 'rep')), may hold values from -6 to 6
- camera_local: int32 [8388608], P(('obs', 'rep')), may hold values from 0 to 1023
- bucket_counts: int32 [256, 64], P(('obs', 'rep')), may hold values from 1 to 512, as said below
- camera_map: int32 [65536], replicated, may hold values from 0 to 65535, each once
Outputs:
- gradient: float32 [9, 65536], replicated
- camera_blocks: float32 [81, 65536], P(None, 'obs')
Inputs may be any that keep to these rules, and one draw needn't show every extreme that they name: bucket_counts[s, d] counts the leading live slots of bucket d of source block s; exactly one destination d has all 512 slots live from every source block, and every other bucket has at most 256 live slots. A slot in bucket d names camera slot d * 1024 + camera_local. `camera_map`: each camera id appears once.
All inputs are finite; a program needn't handle non-finite values.
Results may differ from a plain program's by a relative error of at most 0.0003.
Values sent between devices are 32-bit elements; how exact they have to be, the bound alone decides.
A program may use at most 192 MiB of HBM per device.

v0:
```python
import math

import jax
import jax.numpy as jnp
from jax import lax
from jax.sharding import Mesh
from jax.sharding import PartitionSpec as P

CAM_DEV = 1024
OBS = ("obs_0", "obs_1", "obs_2")
OBS_REP = ("obs_0", "obs_1", "obs_2", "rep")


def sent_together(arrays, axis, split_dim, concat_dim, along):
    widths = [a.shape[along] for a in arrays]
    both = jnp.concatenate(arrays, axis=along)
    filled = lax.all_to_all(both, axis, split_axis=split_dim, concat_axis=concat_dim, tiled=True)
    return tuple(jnp.split(filled, [sum(widths[:k]) for k in range(1, len(widths))], axis=along))


def split_up(shard, dim, count):
    shape = shard.shape
    pieces = shard.reshape(*shape[:dim], count, shape[dim] // count, *shape[dim + 1 :])
    return jnp.moveaxis(pieces, dim, 0)


def summed_on_arrival(shard, axis, dim):
    pieces = split_up(shard, dim, lax.axis_size(axis))
    arrived = lax.all_to_all(pieces, axis, split_axis=0, concat_axis=0, tiled=True)
    return arrived.sum(axis=0)


def side_by_side(arrays, axis, dim, along):
    both = jnp.concatenate(arrays, axis=along)
    filled, at, finished = (summed_on_arrival(both, axis, dim), 0, [])
    for a in arrays:
        finished.append(lax.slice_in_dim(filled, at, at + a.shape[along], axis=along))
        at += a.shape[along]
    return tuple(finished)


def in_order(pieces, dim):
    shape = list(pieces.shape[1:])
    shape[dim] *= pieces.shape[0]
    return jnp.moveaxis(pieces, 0, dim).reshape(shape)


def stacked_from(shard, axes, order):
    pieces = shard[None]
    for k in order:
        pieces = lax.all_gather(pieces, axes[k], axis=0, tiled=True)
    carried = [lax.axis_size(axes[k]) for k in reversed(order)]
    pieces = pieces.reshape(*carried, *shard.shape)
    turned = sorted(range(len(order)), key=lambda place: order[len(order) - 1 - place])
    return pieces.transpose(*turned, *range(len(order), pieces.ndim)).reshape(-1, *shard.shape)


def whole_of(shard, axes, order, dim):
    return in_order(stacked_from(shard, axes, order), dim)


def sent_to_all(shard, axis):
    count = lax.axis_size(axis)
    return lax.all_to_all(
        jnp.broadcast_to(shard[None], (count, *shard.shape)), axis, 0, 0, tiled=True
    )


def gather_directly(shard, axis, dim):
    return in_order(sent_to_all(shard, axis), dim)


def observation_terms(jacobs, resids):
    leading_row = jacobs[0:9]
    trailing_row = jacobs[9:18]
    gradient_terms = leading_row * resids[0:1] + trailing_row * resids[1:2]
    block_terms = (
        leading_row[:, None] * leading_row[None, :] + trailing_row[:, None] * trailing_row[None, :]
    )
    block_terms = block_terms.reshape((81,) + leading_row.shape[1:])
    return jnp.concatenate([gradient_terms, block_terms], axis=0)


def grouped_sums(jac_flat, res_flat, ids_flat, live_flat, width):
    total = jac_flat.shape[1]
    groups = total // width
    camera_rows = lax.broadcasted_iota(jnp.int32, (CAM_DEV, 1), 0)

    def add_group(index, summed):
        start = index * width
        jac_piece = lax.dynamic_slice_in_dim(jac_flat, start, width, 1)
        res_piece = lax.dynamic_slice_in_dim(res_flat, start, width, 1)
        id_piece = lax.dynamic_slice_in_dim(ids_flat, start, width, 0)
        live_piece = lax.dynamic_slice_in_dim(live_flat, start, width, 0)[None, :]
        terms = observation_terms(jac_piece * live_piece, res_piece * live_piece)
        one_hot = (id_piece[None, :] == camera_rows).astype(jnp.float32)
        added = lax.dot_general(
            terms,
            one_hot,
            (((1,), (1,)), ((), ())),
            precision=lax.Precision.HIGHEST,
            preferred_element_type=jnp.float32,
        )
        return summed + added

    return lax.fori_loop(0, groups, add_group, jnp.zeros((90, CAM_DEV), jnp.float32))


def group_width(senders, width):
    return math.gcd(senders, max(1, 2048 // width)) * width


def local(jacobians, residuals, camera_local, bucket_counts, camera_map):
    senders = lax.axis_size(OBS)
    capacity = jacobians.shape[1] // senders
    jac_split = jacobians.reshape(18, senders, capacity)
    res_split = residuals.reshape(2, senders, capacity)
    ids_split = camera_local.reshape(1, senders, capacity)
    counts_here = bucket_counts.reshape(1, senders, 1)
    moved_jac, moved_res = sent_together((jac_split, res_split), OBS, 1, 1, 0)
    moved_ids, moved_counts = sent_together((ids_split, counts_here), OBS, 1, 1, 2)
    within = lax.broadcasted_iota(jnp.int32, (1, senders, capacity), 2)
    live_mask = (within < moved_counts).astype(jnp.float32)
    summed = grouped_sums(
        moved_jac.reshape(18, senders * capacity),
        moved_res.reshape(2, senders * capacity),
        moved_ids.reshape(senders * capacity),
        live_mask.reshape(senders * capacity),
        group_width(senders, capacity),
    )
    grad_part = summed[:9]
    block_part = summed[9:]
    grad_share, block_share = side_by_side((grad_part, block_part), "rep", 1, 0)
    grad_slots = whole_of(grad_share, OBS_REP, (0, 1, 3, 2), 1)
    blocks_out = gather_directly(block_share, "rep", 1)
    gradient = (
        jnp.zeros(grad_slots.shape, jnp.float32)
        .at[:, camera_map]
        .set(grad_slots, unique_indices=True)
    )
    return (gradient, blocks_out)


def solution(mesh):
    split = Mesh(
        mesh.devices.reshape(8, 4, 2, mesh.shape["rep"]), ("obs_0", "obs_1", "obs_2", "rep")
    )
    return jax.shard_map(
        local,
        mesh=split,
        in_specs=(P(None, OBS_REP), P(None, OBS_REP), P(OBS_REP), P(OBS_REP, None), P()),
        out_specs=(P(), P(None, OBS)),
        check_vma=False,
    )
```

profile of v0, /device:TPU:1, one launch (start us, length us, event | category | flops | bytes accessed | tf_op | source)
XLA Modules:
  0.0 553.7 jit_solution(11730834584020948406)
XLA Ops:
  7.2 0.9 reshape.81
  8.9 0.8 copy.22
  9.7 13.1 %all-to-all-start.1 = ((s32[1,64,513]{2,0,1:T(1,128)}), s32[1,64,513]{2,0,1:T(1,128)S(1)}, u32[]{:S(2)}, u32[]{:S(2)}) async-start(s32[1,64,513]{2,0,1:T(1,128)} %copy.22), calls=%async_computation.1 | async-start | bytes 327680 | tf_op jit(solution)/shard_map/all_to_all | solution.py:17
  22.8 3.7 copy.30
  27.9 3.2 copy.19
  31.1 3.4 all-to-all-done.1
  34.5 6.9 %all-to-all-start = ((f32[20,64,512]{2,0,1:T(8,128)}), f32[20,64,512]{2,0,1:T(8,128)S(1)}, u32[]{:S(2)}, u32[]{:S(2)}) async-start(f32[20,64,512]{2,0,1:T(8,128)} %copy.19), calls=%async_computation | async-start | bytes 6291456 | tf_op jit(solution)/shard_map/all_to_all | solution.py:17
  41.7 1.3 slice_reduce_fusion
  43.8 70.0 %all-to-all-done = f32[20,64,512]{2,0,1:T(8,128)S(1)} async-done(((f32[20,64,512]{2,0,1:T(8,128)}), f32[20,64,512]{2,0,1:T(8,128)S(1)}, u32[]{:S(2)}, u32[]{:S(2)}) %all-to-all-start) | async-done | bytes 2621472 | tf_op jit(solution)/shard_map/all_to_all | solution.py:17
  113.9 1.4 copy.20
  115.7 3.5 copy.32
  119.3 118.1 %while.14 = (s32[]{:T(128)}, f32[90,1024]{1,0:T(8,128)}, f32[18,32768]{1,0:T(8,128)}, f32[32768]{0:T(1024)}, f32[2,32768]{1,0:T(2,128)S(1)}, /*index=5*/s32[3276...) while((s32[]{:T(128)}, f32[90,1024]{1,0:T(8,128)}, f32[18,32768]{1,0:T(8,128)}, ...), condition=%wide.region_1.0_spmd.clone, body=%wide.region_0.0_spmd.clone.sunk | while | flops 2267983872 | bytes 7364837 | solution.py:106
  119.3 0.8 dynamic_slice.41
  120.1 1.0 dynamic-slice_multiply_fusion.5
  121.4 4.6 fusion.17
  126.7 0.7 dynamic_slice.41
  127.5 1.0 dynamic-slice_multiply_fusion.5
  128.8 4.6 fusion.17
  134.1 0.7 dynamic_slice.41
  134.9 1.0 dynamic-slice_multiply_fusion.5
  136.1 4.6 fusion.17
  141.4 0.7 dynamic_slice.41
  142.2 1.0 dynamic-slice_multiply_fusion.5
  143.5 4.6 fusion.17
  149.6 1.0 dynamic-slice_multiply_fusion.5
  150.9 4.6 fusion.17
  157.0 1.0 dynamic-slice_multiply_fusion.5
  158.3 4.6 fusion.17
  164.4 1.0 dynamic-slice_multiply_fusion.5
  165.6 4.6 fusion.17
  171.7 1.0 dynamic-slice_multiply_fusion.5
  173.0 4.6 fusion.17
  179.1 1.0 dynamic-slice_multiply_fusion.5
  180.4 4.6 fusion.17
  186.5 1.0 dynamic-slice_multiply_fusion.5
  187.8 4.6 fusion.17
  193.9 1.0 dynamic-slice_multiply_fusion.5
  195.2 4.6 fusion.17
  201.3 1.0 dynamic-slice_multiply_fusion.5
  202.5 4.6 fusion.17
  207.8 0.7 dynamic_slice.41
  208.6 1.0 dynamic-slice_multiply_fusion.5
  209.9 4.6 fusion.17
  216.0 1.0 dynamic-slice_multiply_fusion.5
  217.3 4.6 fusion.17
  223.4 1.0 dynamic-slice_multiply_fusion.5
  224.7 4.6 fusion.17
  230.8 1.0 dynamic-slice_multiply_fusion.5
  232.0 4.6 fusion.17
  237.3 1.2 reshape.85
  238.6 10.0 %all_to_all.20 = f32[4,90,256]{2,1,0:T(8,128)S(1)} all-to-all(f32[4,90,256]{2,1,0:T(8,128)S(1)} %copy.23), channel_id=1, replica_groups=mesh['obs_0'=8,'obs_1'=4,'obs_2'=2,'rep'=4] {'rep'}, dimensions={0} | all-to-all | bytes 737280 | tf_op jit(solution)/shard_map/all_to_all | solution.py:29
  248.7 21.8 %all-gather.1 = f32[8,9,256]{2,1,0:T(8,128)S(1)} all-gather(f32[1,9,256]{2,1,0:T(8,128)S(1)} %slice_bitcast_fusion), channel_id=2, replica_groups=mesh['obs_0'=8,'obs_1'=4,'obs_2'=2,'rep'=4] {'obs_0'}, dimensions={0}, use_global_device_ids=true | all-gather | bytes 82944 | tf_op jit(solution)/shard_map/all_gather | solution.py:51
  270.6 10.2 %all_gather.13 = f32[32,9,256]{2,0,1:T(8,128)} all-gather(f32[8,9,256]{2,0,1:T(8,128)S(1)} %copy.24), channel_id=1, replica_groups=mesh['obs_0'=8,'obs_1'=4,'obs_2'=2,'rep'=4] {'obs_1'}, dimensions={0}, use_global_device_ids=true | all-gather | bytes 368640 | tf_op jit(solution)/shard_map/all_gather | solution.py:51
  280.8 28.4 %all-gather.5.cloned.1.call-done = f32[128,9,256]{2,0,1:T(8,128)} async-done(((f32[32,9,256]{2,0,1:T(8,128)}), f32[128,9,256]{2,0,1:T(8,128)}) %all-gather.5.cloned.1.call-update) | async-done | bytes 1179664 | tf_op jit(solution)/shard_map/all_gather | solution.py:51
  309.2 0.8 broadcast_in_dim.40
  310.0 3.7 all-to-all-start.3
  313.7 6.0 %all-to-all-done.3 = f32[4,81,256]{2,1,0:T(8,128)S(1)} async-done(((f32[4,81,256]{2,1,0:T(8,128)}), f32[4,81,256]{2,1,0:T(8,128)S(1)}, u32[]{:S(2)}, u32[]{:S(2)}) %all-to-all-start.3) | async-done | bytes 331808 | tf_op jit(solution)/shard_map/all_to_all | solution.py:64
  319.9 0.8 copy.34
  320.7 10.1 %all-gather.7.cloned.1.call-done = f32[256,9,256]{2,0,1:T(8,128)} async-done(((f32[128,9,256]{2,0,1:T(8,128)}), f32[256,9,256]{2,0,1:T(8,128)}) %all-gather.7.cloned.1.call-update) | async-done | bytes 2359312 | tf_op jit(solution)/shard_map/all_gather | solution.py:51
  330.8 4.6 copy.37
  335.4 2.7 reshape.87
  338.1 16.6 %copy.29 = f32[9,256,256]{0,2,1:T(8,128)} copy(f32[9,256,256]{2,1,0:T(8,128)S(1)} %bitcast.45) | data formatting | bytes 4718592 | tf_op jit(solution)/shard_map/reshape | solution.py:45
  354.7 172.8 %scatter_custom_fusion = f32[9,65536]{0,1:T(8,128)} fusion(s32[65536]{0:T(1024)S(1)} %compare_select_fusion, f32[65536,9]{1,0:T(8,128)} %bitcast.41, f32[]{:T(128)} %constant.34.clone.1), kind=kCustom, calls=%fused_computation.14 | custom fusion | bytes 2359808 | tf_op jit(solution)/shard_map/scatter | solution.py:139
  527.5 19.4 %copy.28 = f32[9,65536]{1,0:T(8,128)} copy(f32[9,65536]{0,1:T(8,128)} %scatter_custom_fusion) | data formatting | bytes 4718592
  (203 shorter events, 29.1 us)
Async XLA Ops:
  9.7 24.8 %all-to-all-start.1 = ((s32[1,64,513]{2,0,1:T(1,128)}), s32[1,64,513]{2,0,1:T(1,128)S(1)}, u32[]{:S(2)}, u32[]{:S(2)}) async-start(s32[1,64,513]{2,0,1:T(1,128)} %copy.22), calls=%async_computation.1 | async-start | bytes 327680 | tf_op jit(solution)/shard_map/all_to_all | solution.py:17
  26.6 1.0 copy-start.3
  34.5 7.2 %copy-start = (s32[1,64,513]{2,0,1:T(1,128)}, s32[1,64,513]{2,0,1:T(1,128)S(1)}, u32[]{:S(2)}) copy-start(s32[1,64,513]{2,0,1:T(1,128)S(1)} %all-to-all-done.1) | copy-start | bytes 393988
  34.5 79.4 %all-to-all-start = ((f32[20,64,512]{2,0,1:T(8,128)}), f32[20,64,512]{2,0,1:T(8,128)S(1)}, u32[]{:S(2)}, u32[]{:S(2)}) async-start(f32[20,64,512]{2,0,1:T(8,128)} %copy.19), calls=%async_computation | async-start | bytes 6291456 | tf_op jit(solution)/shard_map/all_to_all | solution.py:17
  41.4 267.8 %all-gather.5.cloned.1.call-start = ((), (), s32[]{:S(2)}) async-start(), calls=%async_computation.4 | async-start | bytes 1474560 | tf_op jit(solution)/shard_map/all_gather | solution.py:51
  115.6 3.6 slice-start
  119.3 2.1 copy-start.1
  125.9 0.7 copy-start.2
  126.7 2.1 copy-start.1
  133.3 0.7 copy-start.2
  134.1 2.1 copy-start.1
  140.7 0.7 copy-start.2
  141.4 2.1 copy-start.1
  148.1 0.7 copy-start.2
  148.8 2.1 copy-start.1
  155.5 0.7 copy-start.2
  156.2 2.1 copy-start.1
  162.8 0.7 copy-start.2
  163.6 2.1 copy-start.1
  170.2 0.7 copy-start.2
  171.0 2.1 copy-start.1
  177.6 0.7 copy-start.2
  178.3 2.1 copy-start.1
  185.0 0.7 copy-start.2
  185.7 2.1 copy-start.1
  192.3 0.7 copy-start.2
  193.1 2.1 copy-start.1
  199.7 0.7 copy-start.2
  200.5 2.1 copy-start.1
  207.1 0.7 copy-start.2
  207.8 2.1 copy-start.1
  214.5 0.7 copy-start.2
  215.2 2.1 copy-start.1
  221.8 0.7 copy-start.2
  222.6 2.1 copy-start.1
  229.2 0.7 copy-start.2
  230.0 2.1 copy-start.1
  236.6 0.7 copy-start.2
  237.3 76.3 %copy-start.4 = (s32[65536]{0:T(1024)S(1)}, s32[65536]{0:T(1024)}, u32[]{:S(2)}) copy-start(s32[65536]{0:T(1024)} %param.11) | copy-start | bytes 786436
  280.8 50.0 %all-gather.7.cloned.1.call-start = ((), (), s32[]{:S(2)}) async-start(), calls=%async_computation.5 | async-start | bytes 3538944 | tf_op jit(solution)/shard_map/all_gather | solution.py:51
  310.0 9.7 %all-to-all-start.3 = ((f32[4,81,256]{2,1,0:T(8,128)}), f32[4,81,256]{2,1,0:T(8,128)S(1)}, u32[]{:S(2)}, u32[]{:S(2)}) async-start(f32[4,81,256]{2,1,0:T(8,128)} %broadcast_in_dim.40), calls=%async_computation.3 | async-start | bytes 720896 | tf_op jit(solution)/shard_map/all_to_all | solution.py:64
Sparse Core Ops, SparseCore 0:
  280.9 28.2 all-gather.4
  311.0 19.7 all-gather.6
where the time goes:
time: 555 us; the launch traced here: 554 us
  local copies, waits for them, and re-layouts  262 us (47%)
  waiting for transfers between devices  118 us (21%)
  matrix products  72.9 us (13%)
  blocking collectives  42 us (8%)
  starting transfers between devices  24 us (4%)
  other arithmetic  19.5 us (4%)
  between operations  14.2 us (3%)
    scatter x1, local copies, waits for them, and re-layouts, local(): gradient = jnp.zeros(grad_slots.shape, jnp.float32).at[:, camera_map].set...  173 us
    all_to_all x2, waiting for transfers between devices, sent_together(): lax.all_to_all(both, axis, split_axis=split_dim, concat_axis=concat_dim,...  73.4 us
    dot_general x16, matrix products, add_group(): lax.dot_general(terms, one_hot, (((1,), (1,)), ((), ())), precision=lax.P...  72.9 us
    all_gather x2, waiting for transfers between devices, stacked_from(): pieces = lax.all_gather(pieces, axes[k], axis=0, tiled=True)  38.4 us
    all_gather x2, blocking collectives, stacked_from(): pieces = lax.all_gather(pieces, axes[k], axis=0, tiled=True)  32 us
    unnamed x16, local copies, waits for them, and re-layouts  28.7 us
    all_to_all x2, starting transfers between devices, sent_together(): lax.all_to_all(both, axis, split_axis=split_dim, concat_axis=concat_dim,...  20.1 us
    reshape x1, local copies, waits for them, and re-layouts, in_order(): return jnp.moveaxis(pieces, 0, dim).reshape(shape)  16.6 us
  transfers between devices with their start and end apart: 5, of which 5 were waited for; matrix products, arithmetic and copies ran while one was open for 2% of the time, Pallas kernels for 0%

commit v1 on v0

v1 whole, which is shorter than its diff:
```python
import functools

import jax
import jax.numpy as jnp
from jax import lax
from jax.experimental import pallas as pl
from jax.experimental.pallas import tpu as pltpu
from jax.sharding import PartitionSpec as P

MESH = pl.DeviceIdType.MESH
F32 = jnp.float32
BF16 = jnp.bfloat16
CAP = 512
HALF = 512
ROWS = 56
MSG = 25
VM = functools.partial(pl.BlockSpec, memory_space=pltpu.VMEM)
SM = functools.partial(pl.BlockSpec, memory_space=pltpu.SMEM)


def place():
    obs = lax.axis_index("obs")
    return obs // 8, (obs // 2) % 4, obs % 2, lax.axis_index("rep")


def bucket_of(z, y, core, x):
    return (2 * x + z % 2) * 8 + y * 2 + core


def terms(jac, res):
    j0, j1, r0, r1 = jac[0:9], jac[9:18], res[0:1], res[1:2]

    def turned(j, k):
        return j[0:8] if k == 0 else j[1:9] if k == 1 else jnp.concatenate([j[k:9], j[0 : k - 1]], axis=0)

    rows = [j0[0:8] * turned(j0, k) + j1[0:8] * turned(j1, k) for k in range(5)]
    last0 = jnp.concatenate([j0[8:9], j0[0:4], j0[0:2], r0], axis=0)
    last1 = jnp.concatenate([j1[8:9], j1[0:4], j1[0:2], r1], axis=0)
    rows.append(j0[8:9] * last0 + j1[8:9] * last1)
    rows.append(j0[0:8] * r0 + j1[0:8] * r1)
    return jnp.concatenate(rows, axis=0)


def weighted(jac, res, ids):
    full = terms(jac, res)
    high = full.astype(BF16).astype(F32)
    both = jnp.concatenate([high, full - high], axis=0)
    upper = ids >= HALF
    weights = jnp.concatenate([jnp.where(upper, 0.0, both), jnp.where(upper, both, 0.0)], axis=0)
    ids = jnp.where(upper, ids - HALF, ids)
    rows = lax.broadcasted_iota(jnp.int32, (HALF, ids.shape[1]), 0).astype(F32)
    hot = jnp.where(rows == ids, 1.0, 0.0).astype(BF16)
    return lax.dot_general(hot, weights.astype(BF16), (((1,), (1,)), ((), ())), preferred_element_type=F32)


def unfolded(acc_ref):
    turned = acc_ref[...].T
    low = turned[0:ROWS] + turned[ROWS : 2 * ROWS]
    high = turned[2 * ROWS : 3 * ROWS] + turned[3 * ROWS : 4 * ROWS]
    return low, high


def prep_kernel(counts, jac, res, cam, msg, acc):
    lane = lax.broadcasted_iota(jnp.int32, (1, 128), 1)

    def body(d, hot):
        live = counts[0, d]
        for h in range(2):
            col = pl.multiple_of(d * CAP + h * 128, 128)
            msg[d, h, 0:18, :] = jac[:, pl.ds(col, 128)]
            msg[d, h, 18:20, :] = res[:, pl.ds(col, 128)]
            ids = cam[pl.ds(d * 4 + h, 1), :]
            msg[d, h, 20:21, :] = jnp.where(lane + h * 128 < live, ids, -1).astype(F32)
        return jnp.where(live == CAP, d, hot)

    hot = lax.fori_loop(0, 64, body, 0)
    col = pl.multiple_of(hot * CAP + 256, 128)
    ids = jnp.concatenate([cam[pl.ds(hot * 4 + 2, 1), :], cam[pl.ds(hot * 4 + 3, 1), :]], axis=1).astype(F32)
    acc[:, 4 * ROWS :] = jnp.zeros((HALF, 256 - 4 * ROWS), F32)
    acc[:, : 4 * ROWS] = weighted(jac[:, pl.ds(col, 256)], res[:, pl.ds(col, 256)], ids)
    low, high = unfolded(acc)
    for t in range(ROWS):
        for q in range(4):
            msg[t, 0, 21 + q : 22 + q, :] = low[t : t + 1, q * 128 : (q + 1) * 128]
            msg[t, 1, 21 + q : 22 + q, :] = high[t : t + 1, q * 128 : (q + 1) * 128]
    for t in range(ROWS, 64):
        msg[t, :, 21:25, :] = jnp.zeros((2, 4, 128), F32)


def device_of(bucket, z):
    zd, y, core = bucket // 8, (bucket // 2) % 4, bucket % 2
    return ((z // 2) * 2 + zd % 2) * 8 + y * 2 + core, zd // 2


def exchange_kernel(msg, got, send_sem, recv_sem):
    z, y, core, x = place()
    me = bucket_of(z, y, core, x)
    barrier = pltpu.get_barrier_semaphore()

    def greet(i, c):
        pl.semaphore_signal(barrier, inc=1, device_id=device_of((me + i) % 64, z), device_id_type=MESH)
        return c

    lax.fori_loop(1, 64, greet, 0)
    pl.semaphore_wait(barrier, 63)

    def copy(to, frm):
        return pltpu.make_async_remote_copy(
            src_ref=msg.at[to],
            dst_ref=got.at[frm],
            send_sem=send_sem.at[to],
            recv_sem=recv_sem.at[frm],
            device_id=device_of(to, z),
            device_id_type=MESH,
        )

    def send(i, c):
        copy((me + i) % 64, me).start()
        return c

    lax.fori_loop(1, 64, send, 0)
    got[me] = msg[me]

    def take(i, c):
        copy((me + 64 - i) % 64, (me + 64 - i) % 64).wait_recv()
        return c

    lax.fori_loop(1, 64, take, 0)

    def sent(i, c):
        copy((me + i) % 64, me).wait_send()
        return c

    lax.fori_loop(1, 64, sent, 0)


def sums_kernel(got, msg, acc):
    acc[...] = jnp.zeros_like(acc)
    chunk = 8

    def body(i, c):
        slabs = [got[i * chunk + s, h] for s in range(chunk) for h in range(2)]
        whole = jnp.concatenate([s[0:21] for s in slabs], axis=1)
        acc[:, : 4 * ROWS] += weighted(whole[0:18], whole[18:20], whole[20:21])
        return c

    lax.fori_loop(0, 64 // chunk, body, 0)
    low, high = unfolded(acc)

    def hot(s, total):
        return total + got[s, :, 21:25, :]

    extra = lax.fori_loop(0, 64, hot, jnp.zeros((2, 4, 128), F32))
    for g in range(4):
        part = low if g < 2 else high
        for h in range(2):
            q = (g % 2) * 2 + h
            msg[g, h, 0:ROWS, :] = part[:, q * 128 : (q + 1) * 128]
            msg[g, h, ROWS : ROWS + 1, :] = extra[g // 2, q : q + 1, :]


def slots_of(z, y, core, x):
    return core * 128 + x * 32 + y * 8 + z, core * 128 + y * 32 + x * 8 + z


def at(z, y, core, x):
    return (z * 8 + y * 2 + core, x)


def gather_peers(z, y, core, x):
    peers = [at((z + i) % 8, y, core, x) for i in range(1, 8)]
    peers += [at(z, (y + i) % 4, core, x) for i in range(1, 4)]
    peers += [at(z, y, core, (x + i) % 4) for i in range(1, 4)]
    return peers + [at(z, y, 1 - core, x)]


def gather_all(ref, send_sem, recv_sem):
    z, y, core, x = place()
    slots = slots_of(z, y, core, x)
    ys = [at(z, (y + i) % 4, core, x) for i in range(1, 4)]
    xs = [at(z, y, core, (x + i) % 4) for i in range(1, 4)]
    zs = [at((z + i) % 8, y, core, x) for i in range(1, 8)]
    other = [at(z, y, 1 - core, x)]
    phases = [
        (zs, zs, 1),
        (ys, xs, 8),
        (xs, ys, 32),
        (other, other, 128),
    ]
    for n, (peers0, peers1, size) in enumerate(phases):
        for part, peers in ((0, peers0), (1, peers1)):
            base = (slots[part] // size) * size
            for peer in peers:
                pltpu.make_async_remote_copy(
                    src_ref=ref.at[part, pl.ds(base, size)],
                    dst_ref=ref.at[part, pl.ds(base, size)],
                    send_sem=send_sem.at[n, part],
                    recv_sem=recv_sem.at[n, part],
                    device_id=peer,
                    device_id_type=MESH,
                ).start()
        for part, peers in ((0, peers0), (1, peers1)):
            whole = ref.at[part, pl.ds(0, size * len(peers))]
            pltpu.make_async_remote_copy(
                src_ref=whole,
                dst_ref=whole,
                send_sem=send_sem.at[n, part],
                recv_sem=recv_sem.at[n, part],
                device_id=peers[0],
                device_id_type=MESH,
            ).wait_recv()
    for n, (peers0, peers1, size) in enumerate(phases):
        for part, peers in ((0, peers0), (1, peers1)):
            whole = ref.at[part, pl.ds(0, size * len(peers))]
            pltpu.make_async_remote_copy(
                src_ref=whole,
                dst_ref=whole,
                send_sem=send_sem.at[n, part],
                recv_sem=recv_sem.at[n, part],
                device_id=peers[0],
                device_id_type=MESH,
            ).wait_send()


def reduce_kernel(msg, grads, blocks, got, mine, send2, recv2, send3, recv3, send4, recv4):
    z, y, core, x = place()
    g, p = z // 2, z % 2
    zd = 2 * x + p
    zx, zp, zg = z // 2, z % 2, z
    barrier = pltpu.get_barrier_semaphore()
    zpeers = [at((z + 2 * i) % 8, y, core, x) for i in range(1, 4)]
    greeted = gather_peers(z, y, core, x)
    for peer in greeted:
        pl.semaphore_signal(barrier, inc=1, device_id=peer, device_id_type=MESH)
    owners = [(zd, xo) for xo in range(4)]
    holders = [2 * gg + z % 2 for gg in range(4)]
    count = 14
    for xo in range(4):
        away = jnp.logical_or(zd != z, xo != x)

        @pl.when(away)
        def _():
            pl.semaphore_signal(barrier, inc=1, device_id=at(zd, y, core, xo), device_id_type=MESH)

        count += away.astype(jnp.int32)
    for gg in range(4):
        zh = 2 * gg + zp
        away = jnp.logical_or(zh != z, zx != x)

        @pl.when(away)
        def _():
            pl.semaphore_signal(barrier, inc=1, device_id=at(zh, y, core, zx), device_id_type=MESH)

        count += away.astype(jnp.int32)
    pl.semaphore_wait(barrier, count)

    copies = []
    for i in range(1, 4):
        to = (g + i) % 4
        copies.append(
            pltpu.make_async_remote_copy(
                src_ref=msg.at[to],
                dst_ref=got.at[i],
                send_sem=send2.at[i],
                recv_sem=recv2.at[i],
                device_id=at(2 * to + p, y, core, x),
                device_id_type=MESH,
            )
        )
        copies[-1].start()
    total = msg[g]
    for c in copies:
        c.wait_recv()
    total = total + got[1] + got[2] + got[3]
    mine[...] = total
    slots = slots_of(z, y, core, x)
    for h in range(2):
        grads[h, slots[h]] = total[h, 47:57, :]

    def block_copy(zo, xo, quarter, n):
        return pltpu.make_async_remote_copy(
            src_ref=mine.at[:, pl.ds(0, 45)],
            dst_ref=blocks.at[quarter],
            send_sem=send3.at[n],
            recv_sem=recv3.at[quarter],
            device_id=at(zo, y, core, xo),
            device_id_type=MESH,
        )

    for xo in range(4):
        away = jnp.logical_or(zd != z, xo != x)

        @pl.when(away)
        def _():
            block_copy(zd, xo, g, xo).start()

        @pl.when(jnp.logical_not(away))
        def _():
            blocks[g] = mine[:, 0:45]

    gather_all(grads, send4, recv4)
    for gg in range(4):
        away = jnp.logical_or(2 * gg + zp != z, zx != x)

        @pl.when(away)
        def _():
            block_copy(zd, 0, gg, 0).wait_recv()

    for xo in range(4):
        away = jnp.logical_or(zd != z, xo != x)

        @pl.when(away)
        def _():
            block_copy(zd, xo, g, xo).wait_send()

    for c in copies:
        c.wait_send()


def inverse_kernel(cam_map, out):
    z, y, core, x = place()
    base = (lax.axis_index("obs") * 4 + lax.axis_index("rep")) * 256
    out[...] = jnp.zeros_like(out)
    lane = lax.broadcasted_iota(jnp.int32, (1, 128), 1)
    rows = lax.broadcasted_iota(jnp.int32, (16, 128), 0)
    chunk = 16

    def body(i, acc):
        left, right = [], []
        for k in range(chunk):
            r = i * chunk + k
            place_ = cam_map[pl.ds(r, 1), :] - base
            cam = r * 128 + lane
            inside = jnp.where((place_ >= 0) & (place_ < 256), place_, -16)
            hi, lo = inside >> 4, inside & 15
            hit = rows == hi
            left.append(
                jnp.concatenate(
                    [jnp.where(hit, (cam >> 8).astype(F32), 0.0), jnp.where(hit, (cam & 255).astype(F32), 0.0)], axis=0
                )
            )
            right.append(jnp.where(rows == lo, 1.0, 0.0))
        a = jnp.concatenate(left, axis=1).astype(BF16)
        b = jnp.concatenate(right, axis=1).astype(BF16)
        return acc + lax.dot_general(a, b, (((1,), (1,)), ((), ())), preferred_element_type=F32)

    acc = lax.fori_loop(0, 512 // chunk, body, jnp.zeros((32, 16), F32))
    out[:, 0:16] = (acc[0:16] * 256.0 + acc[16:32]).astype(jnp.int32)


def slot_of_camera(d, g):
    zd = d // 8
    return slots_of(2 * g + zd % 2, (d // 2) % 4, d % 2, zd // 2)


def pick_kernel(counts, inv, grads, out, table):
    def find(d, hot):
        return jnp.where(counts[0, d] == CAP, d, hot)

    hot = lax.fori_loop(0, 64, find, 0)
    out[...] = jnp.zeros_like(out)
    for g in range(4):
        hot_slots = slot_of_camera(hot, g)
        for h in range(2):
            extra = [grads[h, slot_of_camera(47 + k, g)[h], 9:10, :] for k in range(9)]
            table[g * 2 + h, 0:9, :] = grads[h, hot_slots[h], 0:9, :] + jnp.concatenate(extra, axis=0)
    lane = lax.broadcasted_iota(jnp.int32, (1, 128), 1)
    for part in range(2):

        def body(q, acc):
            cam = inv[part * 8 + q // 16, q % 16]
            d, g, h, at_lane = cam // 1024, (cam // 256) % 4, (cam // 128) % 2, cam % 128
            slots = slot_of_camera(d, g)
            slot = jnp.where(h == 0, slots[0], slots[1])
            plain = grads[h, slot, 0:9, :]
            fixed = table[g * 2 + h, 0:9, :]
            tile = jnp.where(d == hot, fixed, plain)
            tile = pltpu.roll(tile, (q - at_lane) % 128, 1)
            return jnp.where(lane == q, tile, acc)

        acc = lax.fori_loop(0, 128, body, jnp.zeros((9, 128), F32))
        out[part] = jnp.concatenate([acc[1:9], acc[0:1]], axis=0)


def spread_kernel(mine, table, send_sem, recv_sem):
    z, y, core, x = place()
    barrier = pltpu.get_barrier_semaphore()
    peers = gather_peers(z, y, core, x)
    for peer in peers:
        pl.semaphore_signal(barrier, inc=1, device_id=peer, device_id_type=MESH)
    pl.semaphore_wait(barrier, len(peers))
    slots = slots_of(z, y, core, x)
    for h in range(2):
        table[h, slots[h]] = mine[h]
    gather_all(table, send_sem, recv_sem)


def finish_kernel(counts, table, grads, blocks, out, blocks_out):
    def place_block(i, c):
        obs, x = i // 4, i % 4
        slots = slots_of(obs // 8, (obs // 2) % 4, obs % 2, x)
        for h in range(2):
            col = pl.multiple_of(i * 256 + h * 128, 128)
            out[:, pl.ds(col, 128)] = table[h, slots[h]]
        return c

    lax.fori_loop(0, 256, place_block, 0)
    hot = counts[0, lax.axis_index("obs")] == CAP
    for g in range(4):
        for h in range(2):
            extra = [grads[h, slot_of_camera(t, g)[h], 9:10, :] for t in range(45)]
            whole = blocks[g, h] + jnp.where(hot, jnp.concatenate(extra, axis=0), 0.0)
            col = g * 256 + h * 128
            for k in range(9):
                for j in range(5):
                    l = (k + j) % 9
                    t = 40 + j if k == 8 else j * 8 + k
                    blocks_out[k * 9 + l : k * 9 + l + 1, col : col + 128] = whole[t : t + 1]
                    if j:
                        blocks_out[l * 9 + k : l * 9 + k + 1, col : col + 128] = whole[t : t + 1]


def shape(*dims, dtype=F32):
    return jax.ShapeDtypeStruct(dims, dtype)


def call(kernel, out, ins, scratch=(), cid=None, **kw):
    params = dict(vmem_limit_bytes=60 * 1024 * 1024)
    if cid is not None:
        params.update(collective_id=cid, has_side_effects=True)
    many = isinstance(out, tuple)
    return pl.pallas_call(
        kernel,
        out_shape=out,
        in_specs=ins,
        out_specs=tuple(VM() for _ in out) if many else VM(),
        scratch_shapes=list(scratch),
        compiler_params=pltpu.CompilerParams(**params),
        **kw,
    )


def local(jacobians, residuals, camera_local, bucket_counts, camera_map):
    dma = pltpu.SemaphoreType.DMA
    cam = camera_local.reshape(256, 128)
    msg = call(
        prep_kernel,
        shape(64, 2, MSG, 128),
        [SM(), VM(), VM(), VM()],
        [pltpu.VMEM((HALF, 256), F32)],
    )(bucket_counts, jacobians, residuals, cam)
    got = call(exchange_kernel, shape(64, 2, MSG, 128), [VM()], [dma((64,)), dma((64,))], cid=1)(msg)
    part = call(sums_kernel, shape(4, 2, ROWS + 1, 128), [VM()], [pltpu.VMEM((HALF, 256), F32)])(got)
    grads, blocks = call(
        reduce_kernel,
        (shape(2, 256, 10, 128), shape(4, 2, 45, 128)),
        [VM()],
        [
            pltpu.VMEM((4, 2, ROWS + 1, 128), F32),
            pltpu.VMEM((2, ROWS + 1, 128), F32),
            dma((4,)),
            dma((4,)),
            dma((4,)),
            dma((4,)),
            dma((4, 2)),
            dma((4, 2)),
        ],
        cid=2,
    )(part)
    inv = call(inverse_kernel, shape(16, 128, dtype=jnp.int32), [VM()])(camera_map.reshape(512, 128))
    mine = call(
        pick_kernel, shape(2, 9, 128), [SM(), SM(), VM()], [pltpu.VMEM((8, 16, 128), F32)]
    )(bucket_counts, inv, grads)
    table = call(spread_kernel, shape(2, 256, 9, 128), [VM()], [dma((4, 2)), dma((4, 2))], cid=3)(mine)
    return call(
        finish_kernel, (shape(9, 65536), shape(81, 1024)), [SM(), VM(), VM(), VM()]
    )(bucket_counts, table, grads, blocks)


def solution(mesh):
    return jax.shard_map(
        local,
        mesh=mesh,
        in_specs=(P(None, ("obs", "rep")), P(None, ("obs", "rep")), P(("obs", "rep")), P(("obs", "rep"), None), P()),
        out_specs=(P(), P(None, "obs")),
        check_vma=False,
    )
```

time: 555 us -> 169 us (0.30)
  local copies, waits for them, and re-layouts: 262 us -> 0 us
  Pallas kernels: 0 us -> 168 us
  waiting for transfers between devices: 118 us -> 0 us
  matrix products: 72.9 us -> 0 us
  blocking collectives: 42 us -> 0 us
  starting transfers between devices: 24 us -> 0 us
  other arithmetic: 19.5 us -> 0 us
  between operations: 14.2 us -> 0.66 us
    scatter x1 -> x0, local copies, waits for them, and re-layouts: 173 us -> none  [local(): gradient = jnp.zeros(grad_slots.shape, jnp.float32).at[:, camera_map].set...]
    pallas_call x0 -> x8, Pallas kernels: none -> 168 us  [the longest x1 52.5 us: local(): call(reduce_kernel, (shape(2, 256, 10, 128), shape(4, 2, 45, 128)), [VM()...]
    all_to_all x3 -> x0, waiting for transfers between devices: 79.4 us -> none  [the longest x2 73.4 us: sent_together(): lax.all_to_all(both, axis, split_axis=split_dim, concat_axis=concat_dim,...]
    dot_general x16 -> x0, matrix products: 72.9 us -> none  [add_group(): lax.dot_general(terms, one_hot, (((1,), (1,)), ((), ())), precision=lax.P...]
    all_gather x2 -> x0, waiting for transfers between devices: 38.4 us -> none  [stacked_from(): pieces = lax.all_gather(pieces, axes[k], axis=0, tiled=True)]
    all_gather x2 -> x0, blocking collectives: 32 us -> none  [stacked_from(): pieces = lax.all_gather(pieces, axes[k], axis=0, tiled=True)]
    unnamed x16 -> x0, local copies, waits for them, and re-layouts: 28.7 us -> none
    reshape x7 -> x0, local copies, waits for them, and re-layouts: 27 us -> none  [the longest x1 16.6 us: in_order(): return jnp.moveaxis(pieces, 0, dim).reshape(shape)]
  transfers between devices with their start and end apart: 5 -> 0, of which waited for: 5 -> 0; matrix products, arithmetic and copies ran while one was open for 2% -> 0% of each run, Pallas kernels for 0% -> 0%
where the time goes in v1:
time: 169 us
  Pallas kernels  168 us (99%)
    pallas_call x1, Pallas kernels, local(): call(reduce_kernel, (shape(2, 256, 10, 128), shape(4, 2, 45, 128)), [VM()...  52.5 us
    pallas_call x1, Pallas kernels, local(): call(exchange_kernel, shape(64, 2, MSG, 128), [VM()], [dma((64,)), dma((6...  34.6 us
    pallas_call x1, Pallas kernels, local(): call(spread_kernel, shape(2, 256, 9, 128), [VM()], [dma((4, 2)), dma((4,...  24.9 us
    pallas_call x1, Pallas kernels, local(): call(pick_kernel, shape(2, 9, 128), [SM(), SM(), VM()], [pltpu.VMEM((8, 1...  22.6 us
    pallas_call x1, Pallas kernels, local(): call(finish_kernel, (shape(9, 65536), shape(81, 1024)), [SM(), VM(), VM()...  12.1 us
    pallas_call x1, Pallas kernels, local(): call(sums_kernel, shape(4, 2, ROWS + 1, 128), [VM()], [pltpu.VMEM((HALF,...  9.44 us
    pallas_call x1, Pallas kernels, local(): call(inverse_kernel, shape(16, 128, dtype=jnp.int32), [VM()])  7.21 us
    pallas_call x1, Pallas kernels, local(): call(prep_kernel, shape(64, 2, MSG, 128), [SM(), VM(), VM(), VM()], [pltp...  4.66 us

profile of v1, /device:TPU:1, one launch (start us, length us, event | category | flops | bytes accessed | tf_op | source)
XLA Modules:
  0.0 168.5 jit_solution(3920424961335520102)
XLA Ops:
  0.6 7.2 %shard_map.68.inv = s32[16,128]{1,0:T(8,128)} custom-call(s32[512,128]{1,0:T(8,128)} %bitcast.2), custom_call_target="tpu_custom_call" | custom-call | tf_op jit(solution)/shard_map/pallas_call | solution.py:470
  7.8 4.7 %shard_map.69.msg = f32[64,2,25,128]{3,2,1,0:T(8,128)} custom-call(s32[1,64]{1,0:T(1,128)} %counts.5, f32[18,32768]{1,0:T(8,128)} %jac.1, f32[2,32768]{1,0:T(2,128)} %res.1, s32[256,128]{1,0:T(8,128)} %bitcast.3), custom_call_target="tpu_custom_call" | custom-call | tf_op jit(solution)/shard_map/pallas_call | solution.py:446
  12.5 34.6 %shard_map.70.got = f32[64,2,25,128]{3,2,1,0:T(8,128)} custom-call(f32[64,2,25,128]{3,2,1,0:T(8,128)} %shard_map.69.msg), custom_call_target="tpu_custom_call" | custom-call | tf_op jit(solution)/shard_map/pallas_call | solution.py:452
  47.1 9.4 %shard_map.71.msg = f32[4,2,57,128]{3,2,1,0:T(8,128)} custom-call(f32[64,2,25,128]{3,2,1,0:T(8,128)} %shard_map.70.got), custom_call_target="tpu_custom_call" | custom-call | tf_op jit(solution)/shard_map/pallas_call | solution.py:453
  56.5 52.5 %shard_map.72 = (f32[2,256,10,128]{3,2,1,0:T(8,128)}, f32[4,2,45,128]{3,2,1,0:T(8,128)}) custom-call(f32[4,2,57,128]{3,2,1,0:T(8,128)} %shard_map.71.msg), custom_call_target="tpu_custom_call" | custom-call | tf_op jit(solution)/shard_map/pallas_call | solution.py:454
  109.0 22.6 %shard_map.73.mine = f32[2,9,128]{2,1,0:T(8,128)} custom-call(s32[1,64]{1,0:T(1,128)} %counts.5, s32[16,128]{1,0:T(8,128)} %shard_map.68.inv, f32[2,256,10,128]{3,2,1,0:T(8,128)} %get-tuple-element.4.grads), custom_call_target="tpu_custom_call" | custom-call | tf_op jit(solution)/shard_map/pallas_call | solution.py:471
  131.6 24.9 %shard_map.74.table = f32[2,256,9,128]{3,2,1,0:T(8,128)} custom-call(f32[2,9,128]{2,1,0:T(8,128)} %shard_map.73.mine), custom_call_target="tpu_custom_call" | custom-call | tf_op jit(solution)/shard_map/pallas_call | solution.py:474
  156.5 12.1 %shard_map.75 = (f32[9,65536]{1,0:T(8,128)}, f32[81,1024]{1,0:T(8,128)}) custom-call(s32[1,64]{1,0:T(1,128)} %counts.5, f32[2,256,9,128]{3,2,1,0:T(8,128)} %shard_map.74.table, f32[2,256,10,128]{3,2,1,0:T(8,128)} %get-tuple-element.4.grads, f32[4,2,45,128]{3,2,1,0:T(8,128)} %get-tuple-element.5.blocks), custom_call_target="tpu_custom_call" | custom-call | tf_op jit(solution)/shard_map/pallas_call | solution.py:475

commit v2 on v0

v2 whole, which is shorter than its diff:
```python
import functools

import jax
import jax.numpy as jnp
from jax import lax
from jax.experimental import pallas as pl
from jax.experimental.pallas import tpu as pltpu
from jax.sharding import PartitionSpec as P

MESH = pl.DeviceIdType.MESH
F32 = jnp.float32
BF16 = jnp.bfloat16
CAP = 512
HALF = 512
ROWS = 56
MSG = 21
SLOTS = 256
VM = functools.partial(pl.BlockSpec, memory_space=pltpu.VMEM)
SM = functools.partial(pl.BlockSpec, memory_space=pltpu.SMEM)


def place():
    obs = lax.axis_index("obs")
    return obs // 8, (obs // 2) % 4, obs % 2, lax.axis_index("rep")


def bucket_of(z, y, core, x):
    return (2 * x + z % 2) * 8 + y * 2 + core


def terms(jac, res):
    j0, j1, r0, r1 = jac[0:9], jac[9:18], res[0:1], res[1:2]

    def turned(j, k):
        return j[0:8] if k == 0 else j[1:9] if k == 1 else jnp.concatenate([j[k:9], j[0 : k - 1]], axis=0)

    rows = [j0[0:8] * turned(j0, k) + j1[0:8] * turned(j1, k) for k in range(5)]
    last0 = jnp.concatenate([j0[8:9], j0[0:4], j0[0:2], r0], axis=0)
    last1 = jnp.concatenate([j1[8:9], j1[0:4], j1[0:2], r1], axis=0)
    rows.append(j0[8:9] * last0 + j1[8:9] * last1)
    rows.append(j0[0:8] * r0 + j1[0:8] * r1)
    return jnp.concatenate(rows, axis=0)


def weighted(jac, res, ids):
    full = terms(jac, res)
    high = full.astype(BF16).astype(F32)
    both = jnp.concatenate([high, full - high], axis=0)
    upper = ids >= HALF
    weights = jnp.concatenate([jnp.where(upper, 0.0, both), jnp.where(upper, both, 0.0)], axis=0)
    ids = jnp.where(upper, ids - HALF, ids)
    rows = lax.broadcasted_iota(jnp.int32, (HALF, ids.shape[1]), 0).astype(F32)
    hot = jnp.where(rows == ids, 1.0, 0.0).astype(BF16)
    return lax.dot_general(hot, weights.astype(BF16), (((1,), (1,)), ((), ())), preferred_element_type=F32)


def unfolded(acc_ref):
    turned = acc_ref[...].T
    low = turned[0:ROWS] + turned[ROWS : 2 * ROWS]
    high = turned[2 * ROWS : 3 * ROWS] + turned[3 * ROWS : 4 * ROWS]
    return low, high


def device_of(bucket, z):
    zd, y, core = bucket // 8, (bucket // 2) % 4, bucket % 2
    return ((z // 2) * 2 + zd % 2) * 8 + y * 2 + core, zd // 2


def slots_of(z, y, core, x):
    return core * 128 + x * 32 + y * 8 + z, core * 128 + y * 32 + x * 8 + z


def slot_of_camera(d, g):
    zd = d // 8
    return slots_of(2 * g + zd % 2, (d // 2) % 4, d % 2, zd // 2)


def at(z, y, core, x):
    return (z * 8 + y * 2 + core, x)


def remote(src, dst, send, recv, device):
    return pltpu.make_async_remote_copy(
        src_ref=src, dst_ref=dst, send_sem=send, recv_sem=recv, device_id=device, device_id_type=MESH
    )


def looped(start, stop, do):
    def body(i, c):
        do(i)
        return c

    lax.fori_loop(start, stop, body, 0)


def camera_ids_here(cam_map, hot):
    base = (lax.axis_index("obs") * 4 + lax.axis_index("rep")) * 256
    lane = lax.broadcasted_iota(jnp.int32, (1, 128), 1)
    rows = lax.broadcasted_iota(jnp.int32, (16, 128), 0)
    chunk = 16

    def body(i, acc):
        left, right = [], []
        for k in range(chunk):
            r = i * chunk + k
            spot = cam_map[pl.ds(r, 1), :] - base
            cam = r * 128 + lane
            inside = jnp.where((spot >= 0) & (spot < 256), spot, -16)
            hit = rows == (inside >> 4)
            left.append(
                jnp.concatenate(
                    [jnp.where(hit, (cam >> 8).astype(F32), 0.0), jnp.where(hit, (cam & 255).astype(F32), 0.0)], axis=0
                )
            )
            right.append(jnp.where(rows == (inside & 15), 1.0, 0.0))
        a = jnp.concatenate(left, axis=1).astype(BF16)
        b = jnp.concatenate(right, axis=1).astype(BF16)
        return acc + lax.dot_general(a, b, (((1,), (1,)), ((), ())), preferred_element_type=F32)

    acc = lax.fori_loop(0, 512 // chunk, body, jnp.zeros((32, 16), F32))
    cam = (acc[0:16] * 256.0 + acc[16:32]).astype(jnp.int32)
    d, g, h, lane = cam >> 10, (cam >> 8) & 3, (cam >> 7) & 1, cam & 127
    zd, y, core = d >> 3, (d >> 1) & 3, d & 1
    slots = slots_of(2 * g + (zd & 1), y, core, zd >> 1)
    spot = jnp.where(h == 0, slots[0], SLOTS + slots[1])
    spot = jnp.where(d == hot, 2 * SLOTS + 2 * g + h, spot)
    return spot * 128 + lane


def front_kernel(
    counts, jac, res, cam, cam_map, part_b, part_g, part_e, inv, msg, hots, gothot, acc, ssem, rsem, hssem, hrsem, *gots
):
    chunk = 64 // len(gots)
    z, y, core, x = place()
    me = bucket_of(z, y, core, x)
    barrier = pltpu.get_barrier_semaphore()
    looped(
        1,
        64,
        lambda i: pl.semaphore_signal(
            barrier, inc=1, device_id=device_of((me + i) % 64, z), device_id_type=MESH
        ),
    )
    lane = lax.broadcasted_iota(jnp.int32, (1, 128), 1)

    def pack(d, carry):
        hot, ejac, eres, eids = carry
        live = counts[0, d]
        for h in range(2):
            col = pl.multiple_of(d * CAP + h * 128, 128)
            msg[d, h, 0:18, :] = jac[:, pl.ds(col, 128)]
            msg[d, h, 18:20, :] = res[:, pl.ds(col, 128)]
            ids = cam[pl.ds(d * 4 + h, 1), :]
            msg[d, h, 20:21, :] = jnp.where(lane + h * 128 < live, ids, -1).astype(F32)
        full = live == CAP
        col = pl.multiple_of(d * CAP + 256, 128)
        ids = jnp.concatenate([cam[pl.ds(d * 4 + 2, 1), :], cam[pl.ds(d * 4 + 3, 1), :]], axis=1)
        return (
            jnp.where(full, d, hot),
            jnp.where(full, jac[:, pl.ds(col, 256)], ejac),
            jnp.where(full, res[:, pl.ds(col, 256)], eres),
            jnp.where(full, ids, eids),
        )

    hot, ejac, eres, eids = lax.fori_loop(
        0,
        64,
        pack,
        (jnp.int32(0), jnp.zeros((18, 256), F32), jnp.zeros((2, 256), F32), jnp.zeros((1, 256), jnp.int32)),
    )
    pl.semaphore_wait(barrier, 63)

    def copy(i):
        to = (me + i) % 64
        return remote(msg.at[to], gots[(i - 1) // chunk].at[(i - 1) % chunk], ssem.at[i], rsem.at[i], device_of(to, z))

    def hot_copy(i):
        to = (me + i) % 64
        return remote(hots.at[to], gothot.at[i], hssem.at[i], hrsem.at[i], device_of(to, z))

    for i in range(1, 64):
        copy(i).start()
    gots[-1][chunk - 1] = msg[me]
    acc[:, 4 * ROWS :] = jnp.zeros((HALF, 256 - 4 * ROWS), F32)
    acc[:, : 4 * ROWS] = weighted(ejac, eres, eids.astype(F32))
    low, high = unfolded(acc)
    for q in range(4):
        hots[0:ROWS, q, :] = low[:, q * 128 : (q + 1) * 128]
        hots[0:ROWS, 4 + q, :] = high[:, q * 128 : (q + 1) * 128]
    hots[ROWS:64] = jnp.zeros((64 - ROWS, 8, 128), F32)
    for i in range(1, 64):
        hot_copy(i).start()
    gothot[0] = hots[me]
    inv[...] = jnp.zeros_like(inv)
    inv[:, 0:16] = camera_ids_here(cam_map, hot)
    inv[0:1, 16:17] = jnp.full((1, 1), hot, jnp.int32)

    acc[...] = jnp.zeros_like(acc)
    for c in range(64 // chunk):
        for i in range(c * chunk + 1, min(c * chunk + chunk + 1, 64)):
            copy(i).wait_recv()
        whole = jnp.concatenate([gots[c][s, h] for s in range(chunk) for h in range(2)], axis=1)
        acc[:, : 4 * ROWS] += weighted(whole[0:18], whole[18:20], whole[20:21])
    low, high = unfolded(acc)
    for i in range(1, 64):
        hot_copy(i).wait_recv()
    extra = lax.fori_loop(0, 64, lambda s, t: t + gothot[s], jnp.zeros((8, 128), F32))
    for g in range(4):
        part = low if g < 2 else high
        for h in range(2):
            q = (g % 2) * 2 + h
            tile = part[:, q * 128 : (q + 1) * 128]
            part_b[g, h] = tile[0:48]
            part_g[g, h] = tile[48:56]
            part_e[g, h, 0:1] = tile[47:48]
            part_e[g, h, 1:2] = extra[g * 2 + h : g * 2 + h + 1]
    for i in range(1, 64):
        copy(i).wait_send()
        hot_copy(i).wait_send()


class Gather:
    def __init__(self, refs, sems):
        self.refs, self.sems = refs, sems
        z, y, core, x = place()
        self.slots = slots_of(z, y, core, x)
        ys = [at(z, (y + i) % 4, core, x) for i in range(1, 4)]
        xs = [at(z, y, core, (x + i) % 4) for i in range(1, 4)]
        self.zs = [at((z + i) % 8, y, core, x) for i in range(1, 8)]
        self.other = at(z, y, 1 - core, x)
        self.middle, self.last = (ys, xs), (xs, ys)
        self.mid, self.far = (y, x), (x, y)
        self.core = core

    def peers(self):
        return self.zs + self.middle[0] + self.middle[1] + [self.other]

    def copies(self, part, start, size, sem, device):
        out = []
        for n, ref in enumerate(self.refs):
            view = ref.at[pl.ds(part * SLOTS + start, size)]
            send, recv = self.sems[n]
            out.append(remote(view, view, send.at[part, sem], recv.at[part, sem], device))
        return out

    def start(self, *args):
        for c in self.copies(*args):
            c.start()

    def wait_recv(self, *args):
        for c in self.copies(*args):
            c.wait_recv()

    def run(self, between=()):
        between = list(between) + [lambda: None] * 3
        for part in range(2):
            for peer in self.zs:
                self.start(part, self.slots[part], 1, 0, peer)
        between[0]()
        blocks = [self.slots[part] // 8 * 8 for part in range(2)]
        for part in range(2):
            self.wait_recv(part, 0, 7, 0, self.zs[0])
            for i in range(3):
                self.start(part, blocks[part], 8, 1 + i, self.middle[part][i])
            for i in range(3):
                self.start(part, blocks[part], 8, 4 + i, self.last[part][i])
            self.start(part, blocks[part], 8, 7, self.other)
        between[1]()
        for i in range(3):
            for part in range(2):
                base = self.core * 128 + self.far[part] * 32 + (self.mid[part] + 3 - i) % 4 * 8
                self.wait_recv(part, base, 8, 1 + i, self.middle[part][i])
                for j in range(3):
                    self.start(part, base, 8, 4 + j, self.last[part][j])
                self.start(part, base, 8, 7, self.other)
        between[2]()
        for j in range(3):
            for part in range(2):
                base = self.core * 128 + (self.far[part] + 3 - j) % 4 * 32
                self.wait_recv(part, base, 32, 4 + j, self.last[part][j])
                self.start(part, base, 32, 7, self.other)
        for part in range(2):
            self.wait_recv(part, 0, 128, 7, self.other)

    def finish(self):
        for part in range(2):
            for sem, size in [(0, 7)] + [(k, 8) for k in (1, 2, 3)] + [(k, 32) for k in (4, 5, 6)] + [(7, 128)]:
                for c in self.copies(part, 0, size, sem, self.other):
                    c.wait_send()


def back_kernel(
    inv, part_b, part_g, part_e, table, table_e, blocks,
    got_b, got_g, got_e, mine_b, bx, bz, grad, grad_e,
    s2b, r2b, s2g, r2g, s2e, r2e, sx, rx, sz, rz, sg, rg, se, re, sg2, rg2, se2, re2,
):
    z, y, core, x = place()
    g, p = z // 2, z % 2
    first = Gather((grad, grad_e), ((sg, rg), (se, re)))
    second = Gather((table, table_e), ((sg2, rg2), (se2, re2)))
    barrier = pltpu.get_barrier_semaphore()
    peers = first.peers()
    for peer in peers:
        pl.semaphore_signal(barrier, inc=1, device_id=peer, device_id_type=MESH)
    pl.semaphore_wait(barrier, len(peers))

    small, large = [], []
    for i in range(1, 4):
        to = (g + i) % 4
        device = at(2 * to + p, y, core, x)
        small.append(remote(part_g.at[to], got_g.at[i - 1], s2g.at[i - 1], r2g.at[i - 1], device))
        small.append(remote(part_e.at[to], got_e.at[i - 1], s2e.at[i - 1], r2e.at[i - 1], device))
        large.append(remote(part_b.at[to], got_b.at[i - 1], s2b.at[i - 1], r2b.at[i - 1], device))
    for c in small + large:
        c.start()
    for c in small:
        c.wait_recv()
    total_g = part_g[g] + got_g[0] + got_g[1] + got_g[2]
    total_e = part_e[g] + got_e[0] + got_e[1] + got_e[2]
    for h in range(2):
        grad[h * SLOTS + first.slots[h]] = total_g[h]
        grad_e[h * SLOTS + first.slots[h]] = total_e[h]

    across, along = [], []
    for i in range(1, 4):
        across.append(remote(mine_b, bx.at[x], sx.at[i - 1], rx.at[i - 1], at(z, y, core, (x + i) % 4)))
        to = (g + i) % 4
        along.append(remote(bx.at[to], bz.at[g], sz.at[i - 1], rz.at[i - 1], at(2 * to + p, y, core, x)))

    def spread_blocks():
        for c in large:
            c.wait_recv()
        mine_b[...] = part_b[g] + got_b[0] + got_b[1] + got_b[2]
        bx[x] = mine_b[...]
        for c in across:
            c.start()

    def send_blocks():
        for c in across:
            c.wait_recv()
        for c in along:
            c.start()
        bz[g] = bx[g]

    first.run([spread_blocks, send_blocks])

    hot = inv[0, 16]
    for gg in range(4):
        hot_slots = slot_of_camera(hot, gg)
        for h in range(2):
            slot = h * SLOTS + hot_slots[h]
            extra = [grad_e[h * SLOTS + slot_of_camera(48 + k, gg)[h], 1:2] for k in range(8)]
            grad[2 * SLOTS + 2 * gg + h] = grad[slot] + jnp.concatenate(extra, axis=0)
            grad_e[2 * SLOTS + 2 * gg + h, 0:1] = (
                grad_e[slot, 0:1] + grad_e[h * SLOTS + slot_of_camera(47, gg)[h], 1:2]
            )
            grad_e[2 * SLOTS + 2 * gg + h, 1:2] = jnp.zeros((1, 128), F32)
    lane = lax.broadcasted_iota(jnp.int32, (1, 128), 1)
    for h in range(2):

        def pick(r, acc):
            top, low = acc
            for k in range(16):
                v = inv[h * 8 + r, k]
                q = r * 16 + k
                turn = (q - v) & 127
                at_q = lane == q
                top = jnp.where(at_q, pltpu.roll(grad[v >> 7], turn, 1), top)
                low = jnp.where(at_q, pltpu.roll(grad_e[v >> 7], turn, 1), low)
            return top, low

        top, low = lax.fori_loop(0, 8, pick, (jnp.zeros((8, 128), F32), jnp.zeros((2, 128), F32)))
        table[h * SLOTS + second.slots[h]] = top
        table_e[h * SLOTS + second.slots[h]] = low[0:1]

    def fix_blocks():
        for c in along:
            c.wait_recv()
        here = lax.axis_index("obs") == hot
        for gg in range(4):
            for h in range(2):
                extra = [grad_e[h * SLOTS + slot_of_camera(t, gg)[h], 1:2] for t in range(45)]
                extra = jnp.concatenate(extra + [jnp.zeros((3, 128), F32)], axis=0)
                blocks[gg, h] = bz[gg, h] + jnp.where(here, extra, 0.0)

    second.run([lambda: None, fix_blocks])
    for c in small + large + across + along:
        c.wait_send()
    first.finish()
    second.finish()


def finish_kernel(table, table_e, blocks, out, blocks_out):
    def place_block(i, c):
        obs, x = i >> 2, i & 3
        slots = slots_of(obs >> 3, (obs >> 1) & 3, obs & 1, x)
        for h in range(2):
            col = pl.multiple_of(i * 256 + h * 128, 128)
            slot = h * SLOTS + slots[h]
            out[0:8, pl.ds(col, 128)] = table[slot]
            out[8:9, pl.ds(col, 128)] = table_e[slot]
        return c

    lax.fori_loop(0, 256, place_block, 0, unroll=8)
    for g in range(4):
        for h in range(2):
            whole = blocks[g, h]
            col = g * 256 + h * 128
            for k in range(9):
                for j in range(5):
                    m = (k + j) % 9
                    t = 40 + j if k == 8 else j * 8 + k
                    blocks_out[k * 9 + m : k * 9 + m + 1, col : col + 128] = whole[t : t + 1]
                    if j:
                        blocks_out[m * 9 + k : m * 9 + k + 1, col : col + 128] = whole[t : t + 1]


def shape(*dims, dtype=F32):
    return jax.ShapeDtypeStruct(dims, dtype)


def call(kernel, out, ins, scratch=(), cid=None, **kw):
    params = dict(vmem_limit_bytes=60 * 1024 * 1024)
    if cid is not None:
        params.update(collective_id=cid, has_side_effects=True)
    many = isinstance(out, tuple)
    return pl.pallas_call(
        kernel,
        out_shape=out,
        in_specs=ins,
        out_specs=tuple(VM() for _ in out) if many else VM(),
        scratch_shapes=list(scratch),
        compiler_params=pltpu.CompilerParams(**params),
        **kw,
    )


def vmem(*dims):
    return pltpu.VMEM(dims, F32)


def local(jacobians, residuals, camera_local, bucket_counts, camera_map):
    dma = pltpu.SemaphoreType.DMA
    part_b, part_g, part_e, inv = call(
        front_kernel,
        (shape(4, 2, 48, 128), shape(4, 2, 8, 128), shape(4, 2, 2, 128), shape(16, 128, dtype=jnp.int32)),
        [SM(), VM(), VM(), VM(), VM()],
        [
            vmem(64, 2, MSG, 128),
            vmem(64, 8, 128),
            vmem(64, 8, 128),
            vmem(HALF, 256),
        ]
        + [dma((64,))] * 4
        + [vmem(8, 2, MSG, 128)] * 8,
        cid=1,
        name="front",
    )(bucket_counts, jacobians, residuals, camera_local.reshape(256, 128), camera_map.reshape(512, 128))
    table, table_e, blocks = call(
        back_kernel,
        (shape(2 * SLOTS, 8, 128), shape(2 * SLOTS, 1, 128), shape(4, 2, 48, 128)),
        [SM(), VM(), VM(), VM()],
        [
            vmem(3, 2, 48, 128),
            vmem(3, 2, 8, 128),
            vmem(3, 2, 2, 128),
            vmem(2, 48, 128),
            vmem(4, 2, 48, 128),
            vmem(4, 2, 48, 128),
            vmem(2 * SLOTS + 8, 8, 128),
            vmem(2 * SLOTS + 8, 2, 128),
        ]
        + [dma((3,))] * 10
        + [dma((2, 8))] * 8,
        cid=2,
        name="back",
    )(inv, part_b, part_g, part_e)
    return call(finish_kernel, (shape(9, 65536), shape(81, 1024)), [VM(), VM(), VM()], name="finish")(
        table, table_e, blocks
    )


def solution(mesh):
    return jax.shard_map(
        local,
        mesh=mesh,
        in_specs=(P(None, ("obs", "rep")), P(None, ("obs", "rep")), P(("obs", "rep")), P(("obs", "rep"), None), P()),
        out_specs=(P(), P(None, "obs")),
        check_vma=False,
    )
```

time: 555 us -> 104 us (0.19)
  local copies, waits for them, and re-layouts: 262 us -> 0 us
  waiting for transfers between devices: 118 us -> 0 us
  Pallas kernels: 0 us -> 103 us
  matrix products: 72.9 us -> 0 us
  blocking collectives: 42 us -> 0 us
  starting transfers between devices: 24 us -> 0 us
  other arithmetic: 19.5 us -> 0 us
  between operations: 14.2 us -> 0.65 us
    scatter x1 -> x0, local copies, waits for them, and re-layouts: 173 us -> none  [local(): gradient = jnp.zeros(grad_slots.shape, jnp.float32).at[:, camera_map].set...]
    pallas_call x0 -> x3, Pallas kernels: none -> 103 us  [the longest x1 57 us: local(): call(back_kernel, (shape(2 * SLOTS, 8, 128), shape(2 * SLOTS, 1, 128), sh...]
    all_to_all x3 -> x0, waiting for transfers between devices: 79.4 us -> none  [the longest x2 73.4 us: sent_together(): lax.all_to_all(both, axis, split_axis=split_dim, concat_axis=concat_dim,...]
    dot_general x16 -> x0, matrix products: 72.9 us -> none  [add_group(): lax.dot_general(terms, one_hot, (((1,), (1,)), ((), ())), precision=lax.P...]
    all_gather x2 -> x0, waiting for transfers between devices: 38.4 us -> none  [stacked_from(): pieces = lax.all_gather(pieces, axes[k], axis=0, tiled=True)]
    all_gather x2 -> x0, blocking collectives: 32 us -> none  [stacked_from(): pieces = lax.all_gather(pieces, axes[k], axis=0, tiled=True)]
    unnamed x16 -> x0, local copies, waits for them, and re-layouts: 28.7 us -> none
    reshape x7 -> x0, local copies, waits for them, and re-layouts: 27 us -> none  [the longest x1 16.6 us: in_order(): return jnp.moveaxis(pieces, 0, dim).reshape(shape)]
  transfers between devices with their start and end apart: 5 -> 0, of which waited for: 5 -> 0; matrix products, arithmetic and copies ran while one was open for 2% -> 0% of each run, Pallas kernels for 0% -> 0%
where the time goes in v2:
time: 104 us
  Pallas kernels  103 us (99%)
    pallas_call x1, Pallas kernels, local(): call(back_kernel, (shape(2 * SLOTS, 8, 128), shape(2 * SLOTS, 1, 128), sh...  57 us
    pallas_call x1, Pallas kernels, local(): call(front_kernel, (shape(4, 2, 48, 128), shape(4, 2, 8, 128), shape(4, 2...  39.7 us
    pallas_call x1, Pallas kernels, local(): call(finish_kernel, (shape(9, 65536), shape(81, 1024)), [VM(), VM(), VM()...  6.34 us

profile of v2, /device:TPU:1, one launch (start us, length us, event | category | flops | bytes accessed | tf_op | source)
XLA Modules:
  0.0 103.7 jit_solution(1353492753562387337)
XLA Ops:
  0.6 39.7 %front.1 = (f32[4,2,48,128]{3,2,1,0:T(8,128)}, f32[4,2,8,128]{3,2,1,0:T(8,128)}, f32[4,2,2,128]{3,2,1,0:T(2,128)}, s32[16,128]{1,0:T(8,128)}) custom-call(s32[1,64]{1,0:T(1,128)} %counts.1, f32[18,32768]{1,0:T(8,128)} %jac.1, f32[2,32768]{1,0:T(2,128)} %res.1, s32[256,128]{1,0:T(8,128)} %bitcast.3, s32[512,128]{1,0:T(8,128)} %bitcast.2), custom_call_target="tpu_custom_call" | custom-call | tf_op jit(solution)/shard_map/front/pallas_call | solution.py:444
  40.4 57.0 %back.1 = (f32[512,8,128]{2,1,0:T(8,128)}, f32[512,1,128]{2,1,0:T(1,128)}, f32[4,2,48,128]{3,2,1,0:T(8,128)}) custom-call(s32[16,128]{1,0:T(8,128)} %get-tuple-element.9.inv, f32[4,2,48,128]{3,2,1,0:T(8,128)} %get-tuple-element.10.part_b, f32[4,2,8,128]{3,2,1,0:T(8,128)} %get-tuple-element.11.part_g, f32[4,2,2,128]{3,2,1,0:T(2,128)} %get-tuple-element.12.part_e), custom_call_target="tpu_custom_call" | custom-call | tf_op jit(solution)/shard_map/back/pallas_call | solution.py:459
  97.4 6.3 %finish.1 = (f32[9,65536]{1,0:T(8,128)}, f32[81,1024]{1,0:T(8,128)}) custom-call(f32[512,8,128]{2,1,0:T(8,128)} %get-tuple-element.13.table, f32[512,1,128]{2,1,0:T(1,128)} %get-tuple-element.14.table_e, f32[4,2,48,128]{3,2,1,0:T(8,128)} %get-tuple-element.15.blocks), custom_call_target="tpu_custom_call" | custom-call | tf_op jit(solution)/shard_map/finish/pallas_call | solution.py:478

commit v3 on v2

--- a/solution.py
+++ b/solution.py
@@ -94,7 +94,8 @@
 
 
 def camera_ids_here(cam_map, hot):
-    base = (lax.axis_index("obs") * 4 + lax.axis_index("rep")) * 256
+    slots = slots_of(*place())
+    bases = (slots[0] * 128, (SLOTS + slots[1]) * 128)
     lane = lax.broadcasted_iota(jnp.int32, (1, 128), 1)
     rows = lax.broadcasted_iota(jnp.int32, (16, 128), 0)
     chunk = 16
@@ -103,9 +104,11 @@
         left, right = [], []
         for k in range(chunk):
             r = i * chunk + k
-            spot = cam_map[pl.ds(r, 1), :] - base
             cam = r * 128 + lane
-            inside = jnp.where((spot >= 0) & (spot < 256), spot, -16)
+            first = cam_map[pl.ds(r, 1), :] - bases[0]
+            second = cam_map[pl.ds(r, 1), :] - bases[1]
+            inside = jnp.where((first >= 0) & (first < 128), first, -16)
+            inside = jnp.where((second >= 0) & (second < 128), second + 128, inside)
             hit = rows == (inside >> 4)
             left.append(
                 jnp.concatenate(
@@ -252,7 +255,7 @@
             c.wait_recv()
 
     def run(self, between=()):
-        between = list(between) + [lambda: None] * 3
+        between = list(between) + [lambda: None] * 4
         for part in range(2):
             for peer in self.zs:
                 self.start(part, self.slots[part], 1, 0, peer)
@@ -279,6 +282,7 @@
                 base = self.core * 128 + (self.far[part] + 3 - j) % 4 * 32
                 self.wait_recv(part, base, 32, 4 + j, self.last[part][j])
                 self.start(part, base, 32, 7, self.other)
+        between[3]()
         for part in range(2):
             self.wait_recv(part, 0, 128, 7, self.other)
 
@@ -311,7 +315,7 @@
         small.append(remote(part_g.at[to], got_g.at[i - 1], s2g.at[i - 1], r2g.at[i - 1], device))
         small.append(remote(part_e.at[to], got_e.at[i - 1], s2e.at[i - 1], r2e.at[i - 1], device))
         large.append(remote(part_b.at[to], got_b.at[i - 1], s2b.at[i - 1], r2b.at[i - 1], device))
-    for c in small + large:
+    for c in small:
         c.start()
     for c in small:
         c.wait_recv()
@@ -327,6 +331,13 @@
         to = (g + i) % 4
         along.append(remote(bx.at[to], bz.at[g], sz.at[i - 1], rz.at[i - 1], at(2 * to + p, y, core, x)))
 
+    def nothing():
+        pass
+
+    def start_blocks():
+        for c in large:
+            c.start()
+
     def spread_blocks():
         for c in large:
             c.wait_recv()
@@ -342,7 +353,7 @@
             c.start()
         bz[g] = bx[g]
 
-    first.run([spread_blocks, send_blocks])
+    first.run([nothing, start_blocks])
 
     hot = inv[0, 16]
     for gg in range(4):
@@ -383,7 +394,7 @@
                 extra = jnp.concatenate(extra + [jnp.zeros((3, 128), F32)], axis=0)
                 blocks[gg, h] = bz[gg, h] + jnp.where(here, extra, 0.0)
 
-    second.run([lambda: None, fix_blocks])
+    second.run([spread_blocks, send_blocks, nothing, fix_blocks])
     for c in small + large + across + along:
         c.wait_send()
     first.finish()
@@ -391,28 +402,19 @@
 
 
 def finish_kernel(table, table_e, blocks, out, blocks_out):
-    def place_block(i, c):
-        obs, x = i >> 2, i & 3
-        slots = slots_of(obs >> 3, (obs >> 1) & 3, obs & 1, x)
-        for h in range(2):
-            col = pl.multiple_of(i * 256 + h * 128, 128)
-            slot = h * SLOTS + slots[h]
-            out[0:8, pl.ds(col, 128)] = table[slot]
-            out[8:9, pl.ds(col, 128)] = table_e[slot]
-        return c
-
-    lax.fori_loop(0, 256, place_block, 0, unroll=8)
-    for g in range(4):
-        for h in range(2):
-            whole = blocks[g, h]
-            col = g * 256 + h * 128
-            for k in range(9):
-                for j in range(5):
-                    m = (k + j) % 9
-                    t = 40 + j if k == 8 else j * 8 + k
-                    blocks_out[k * 9 + m : k * 9 + m + 1, col : col + 128] = whole[t : t + 1]
-                    if j:
-                        blocks_out[m * 9 + k : m * 9 + k + 1, col : col + 128] = whole[t : t + 1]
+    for n in range(table.shape[0]):
+        out[0:8, n * 128 : (n + 1) * 128] = table[n]
+        out[8:9, n * 128 : (n + 1) * 128] = table_e[n]
+    for h in range(2):
+        whole = blocks[0, h]
+        here = slice(h * 128, (h + 1) * 128)
+        for k in range(9):
+            for j in range(5):
+                m = (k + j) % 9
+                t = 40 + j if k == 8 else j * 8 + k
+                blocks_out[k * 9 + m : k * 9 + m + 1, here] = whole[t : t + 1]
+                if j:
+                    blocks_out[m * 9 + k : m * 9 + k + 1, here] = whole[t : t + 1]
 
 
 def shape(*dims, dtype=F32):
@@ -475,9 +477,18 @@
         cid=2,
         name="back",
     )(inv, part_b, part_g, part_e)
-    return call(finish_kernel, (shape(9, 65536), shape(81, 1024)), [VM(), VM(), VM()], name="finish")(
-        table, table_e, blocks
-    )
+    return pl.pallas_call(
+        finish_kernel,
+        out_shape=(shape(9, 65536), shape(81, 1024)),
+        grid=(4,),
+        in_specs=[
+            pl.BlockSpec((2 * SLOTS // 4, 8, 128), lambda n: (n, 0, 0)),
+            pl.BlockSpec((2 * SLOTS // 4, 1, 128), lambda n: (n, 0, 0)),
+            pl.BlockSpec((1, 2, 48, 128), lambda n: (n, 0, 0, 0)),
+        ],
+        out_specs=(pl.BlockSpec((9, 16384), lambda n: (0, n)), pl.BlockSpec((81, 256), lambda n: (0, n))),
+        name="finish",
+    )(table, table_e, blocks)
 
 
 def solution(mesh):

time: 104 us -> 99.9 us (0.961)
  Pallas kernels: 103 us -> 99.1 us
    pallas_call x1, Pallas kernels: 57 us -> 54.8 us  [local(): call(back_kernel, (shape(2 * SLOTS, 8, 128), shape(2 * SLOTS, 1, 128), sh...]
    pallas_call x1, Pallas kernels: 6.34 us -> 4.36 us  [local(): pl.pallas_call(finish_kernel, out_shape=(shape(9, 65536), shape(81, 1024)...]
where the time goes in v3:
time: 99.9 us; the launch traced here: 99.8 us
  Pallas kernels  99.1 us (99%)
    pallas_call x1, Pallas kernels, local(): call(back_kernel, (shape(2 * SLOTS, 8, 128), shape(2 * SLOTS, 1, 128), sh...  54.8 us
    pallas_call x1, Pallas kernels, local(): call(front_kernel, (shape(4, 2, 48, 128), shape(4, 2, 8, 128), shape(4, 2...  39.9 us
    pallas_call x1, Pallas kernels, local(): pl.pallas_call(finish_kernel, out_shape=(shape(9, 65536), shape(81, 1024)...  4.36 us

profile of v3, /device:TPU:1, one launch (start us, length us, event | category | flops | bytes accessed | tf_op | source)
XLA Modules:
  0.0 99.8 jit_solution(13362778626919343089)
XLA Ops:
  0.6 39.9 %front.1 = (f32[4,2,48,128]{3,2,1,0:T(8,128)}, f32[4,2,8,128]{3,2,1,0:T(8,128)}, f32[4,2,2,128]{3,2,1,0:T(2,128)}, s32[16,128]{1,0:T(8,128)}) custom-call(s32[1,64]{1,0:T(1,128)} %counts.1, f32[18,32768]{1,0:T(8,128)} %jac.1, f32[2,32768]{1,0:T(2,128)} %res.1, s32[256,128]{1,0:T(8,128)} %bitcast.3, s32[512,128]{1,0:T(8,128)} %bitcast.2), custom_call_target="tpu_custom_call" | custom-call | tf_op jit(solution)/shard_map/front/pallas_call | solution.py:446
  40.6 54.8 %back.1 = (f32[512,8,128]{2,1,0:T(8,128)}, f32[512,1,128]{2,1,0:T(1,128)}, f32[4,2,48,128]{3,2,1,0:T(8,128)}) custom-call(s32[16,128]{1,0:T(8,128)} %get-tuple-element.9.inv, f32[4,2,48,128]{3,2,1,0:T(8,128)} %get-tuple-element.10.part_b, f32[4,2,8,128]{3,2,1,0:T(8,128)} %get-tuple-element.11.part_g, f32[4,2,2,128]{3,2,1,0:T(2,128)} %get-tuple-element.12.part_e), custom_call_target="tpu_custom_call" | custom-call | tf_op jit(solution)/shard_map/back/pallas_call | solution.py:461
  95.4 4.4 %finish.1 = (f32[9,65536]{1,0:T(8,128)}, f32[81,1024]{1,0:T(8,128)}) custom-call(f32[512,8,128]{2,1,0:T(8,128)} %get-tuple-element.13.table, f32[512,1,128]{2,1,0:T(1,128)} %get-tuple-element.14.table_e, f32[4,2,48,128]{3,2,1,0:T(8,128)} %get-tuple-element.15.blocks), custom_call_target="tpu_custom_call" | custom-call | tf_op jit(solution)/shard_map/finish/pallas_call | solution.py:480

commit v4 on v3

--- a/solution.py
+++ b/solution.py
@@ -121,7 +121,7 @@
         return acc + lax.dot_general(a, b, (((1,), (1,)), ((), ())), preferred_element_type=F32)
 
     acc = lax.fori_loop(0, 512 // chunk, body, jnp.zeros((32, 16), F32))
-    cam = (acc[0:16] * 256.0 + acc[16:32]).astype(jnp.int32)
+    cam = (acc[0:16] * 256.0 + acc[16:32]).astype(jnp.int32) & (256 * SLOTS - 1)
     d, g, h, lane = cam >> 10, (cam >> 8) & 3, (cam >> 7) & 1, cam & 127
     zd, y, core = d >> 3, (d >> 1) & 3, d & 1
     slots = slots_of(2 * g + (zd & 1), y, core, zd >> 1)
@@ -130,8 +130,8 @@
     return spot * 128 + lane
 
 
-def front_kernel(
-    counts, jac, res, cam, cam_map, part_b, part_g, part_e, inv, msg, hots, gothot, acc, ssem, rsem, hssem, hrsem, *gots
+def sum_buckets(
+    counts, jac, res, cam, cam_map, part_b, part_g, part_e, inv, msg, hots, gothot, acc, ssem, rsem, hssem, hrsem, gots
 ):
     chunk = 64 // len(gots)
     z, y, core, x = place()
@@ -144,6 +144,9 @@
             barrier, inc=1, device_id=device_of((me + i) % 64, z), device_id_type=MESH
         ),
     )
+    outside = [at(((z // 2) * 2 + i) % 8, y, core, x) for i in range(2, 8)]
+    for peer in outside:
+        pl.semaphore_signal(barrier, inc=1, device_id=peer, device_id_type=MESH)
     lane = lax.broadcasted_iota(jnp.int32, (1, 128), 1)
 
     def pack(d, carry):
@@ -171,7 +174,7 @@
         pack,
         (jnp.int32(0), jnp.zeros((18, 256), F32), jnp.zeros((2, 256), F32), jnp.zeros((1, 256), jnp.int32)),
     )
-    pl.semaphore_wait(barrier, 63)
+    pl.semaphore_wait(barrier, 63 + len(outside))
 
     def copy(i):
         to = (me + i) % 64
@@ -217,9 +220,13 @@
             part_g[g, h] = tile[48:56]
             part_e[g, h, 0:1] = tile[47:48]
             part_e[g, h, 1:2] = extra[g * 2 + h : g * 2 + h + 1]
-    for i in range(1, 64):
-        copy(i).wait_send()
-        hot_copy(i).wait_send()
+
+    def finish():
+        for i in range(1, 64):
+            copy(i).wait_send()
+            hot_copy(i).wait_send()
+
+    return finish
 
 
 class Gather:
@@ -293,20 +300,22 @@
                     c.wait_send()
 
 
-def back_kernel(
-    inv, part_b, part_g, part_e, table, table_e, blocks,
+def main_kernel(
+    counts, jac, res, cam, cam_map, table, table_e, blocks,
+    part_b, part_g, part_e, found, inv, msg, hots, gothot, acc, ssem, rsem, hssem, hrsem, isem,
     got_b, got_g, got_e, mine_b, bx, bz, grad, grad_e,
     s2b, r2b, s2g, r2g, s2e, r2e, sx, rx, sz, rz, sg, rg, se, re, sg2, rg2, se2, re2,
+    *gots,
 ):
+    sums_sent = sum_buckets(
+        counts, jac, res, cam, cam_map, part_b, part_g, part_e, found, msg, hots, gothot, acc, ssem, rsem, hssem, hrsem, gots
+    )
     z, y, core, x = place()
     g, p = z // 2, z % 2
     first = Gather((grad, grad_e), ((sg, rg), (se, re)))
     second = Gather((table, table_e), ((sg2, rg2), (se2, re2)))
-    barrier = pltpu.get_barrier_semaphore()
-    peers = first.peers()
-    for peer in peers:
-        pl.semaphore_signal(barrier, inc=1, device_id=peer, device_id_type=MESH)
-    pl.semaphore_wait(barrier, len(peers))
+    ids = pltpu.make_async_copy(found, inv, isem)
+    ids.start()
 
     small, large = [], []
     for i in range(1, 4):
@@ -355,6 +364,7 @@
 
     first.run([nothing, start_blocks])
 
+    ids.wait()
     hot = inv[0, 16]
     for gg in range(4):
         hot_slots = slot_of_camera(hot, gg)
@@ -399,6 +409,7 @@
         c.wait_send()
     first.finish()
     second.finish()
+    sums_sent()
 
 
 def finish_kernel(table, table_e, blocks, out, blocks_out):
@@ -443,26 +454,24 @@
 
 def local(jacobians, residuals, camera_local, bucket_counts, camera_map):
     dma = pltpu.SemaphoreType.DMA
-    part_b, part_g, part_e, inv = call(
-        front_kernel,
-        (shape(4, 2, 48, 128), shape(4, 2, 8, 128), shape(4, 2, 2, 128), shape(16, 128, dtype=jnp.int32)),
+    table, table_e, blocks = call(
+        main_kernel,
+        (shape(2 * SLOTS, 8, 128), shape(2 * SLOTS, 1, 128), shape(4, 2, 48, 128)),
         [SM(), VM(), VM(), VM(), VM()],
         [
+            vmem(4, 2, 48, 128),
+            vmem(4, 2, 8, 128),
+            vmem(4, 2, 2, 128),
+            pltpu.VMEM((16, 128), jnp.int32),
+            pltpu.SMEM((16, 128), jnp.int32),
             vmem(64, 2, MSG, 128),
             vmem(64, 8, 128),
             vmem(64, 8, 128),
             vmem(HALF, 256),
         ]
         + [dma((64,))] * 4
-        + [vmem(8, 2, MSG, 128)] * 8,
-        cid=1,
-        name="front",
-    )(bucket_counts, jacobians, residuals, camera_local.reshape(256, 128), camera_map.reshape(512, 128))
-    table, table_e, blocks = call(
-        back_kernel,
-        (shape(2 * SLOTS, 8, 128), shape(2 * SLOTS, 1, 128), shape(4, 2, 48, 128)),
-        [SM(), VM(), VM(), VM()],
-        [
+        + [
+            dma,
             vmem(3, 2, 48, 128),
             vmem(3, 2, 8, 128),
             vmem(3, 2, 2, 128),
@@ -473,10 +482,11 @@
             vmem(2 * SLOTS + 8, 2, 128),
         ]
         + [dma((3,))] * 10
-        + [dma((2, 8))] * 8,
-        cid=2,
-        name="back",
-    )(inv, part_b, part_g, part_e)
+        + [dma((2, 8))] * 8
+        + [vmem(8, 2, MSG, 128)] * 8,
+        cid=1,
+        name="main",
+    )(bucket_counts, jacobians, residuals, camera_local.reshape(256, 128), camera_map.reshape(512, 128))
     return pl.pallas_call(
         finish_kernel,
         out_shape=(shape(9, 65536), shape(81, 1024)),

time: 99.9 us -> 97.9 us (0.980)
  Pallas kernels: 99.1 us -> 97.1 us
    pallas_call x2 -> x1, Pallas kernels: 94.8 us -> 92.8 us  [local(): call(main_kernel, (shape(2 * SLOTS, 8, 128), shape(2 * SLOTS, 1, 128), sh...]
where the time goes in v4:
time: 97.9 us; the launch traced here: 97.8 us
  Pallas kernels  97.1 us (99%)
    pallas_call x1, Pallas kernels, local(): call(main_kernel, (shape(2 * SLOTS, 8, 128), shape(2 * SLOTS, 1, 128), sh...  92.8 us
    pallas_call x1, Pallas kernels, local(): pl.pallas_call(finish_kernel, out_shape=(shape(9, 65536), shape(81, 1024)...  4.36 us

profile of v4, /device:TPU:1, one launch (start us, length us, event | category | flops | bytes accessed | tf_op | source)
XLA Modules:
  0.0 97.8 jit_solution(18201843348700019704)
XLA Ops:
  0.6 92.8 %main.1 = (f32[512,8,128]{2,1,0:T(8,128)}, f32[512,1,128]{2,1,0:T(1,128)}, f32[4,2,48,128]{3,2,1,0:T(8,128)}) custom-call(s32[1,64]{1,0:T(1,128)} %counts.1, f32[18,32768]{1,0:T(8,128)} %jac.1, f32[2,32768]{1,0:T(2,128)} %res.1, s32[256,128]{1,0:T(8,128)} %bitcast.3, s32[512,128]{1,0:T(8,128)} %bitcast.2), custom_call_target="tpu_custom_call" | custom-call | tf_op jit(solution)/shard_map/main/pallas_call | solution.py:457
  93.4 4.4 %finish.1 = (f32[9,65536]{1,0:T(8,128)}, f32[81,1024]{1,0:T(8,128)}) custom-call(f32[512,8,128]{2,1,0:T(8,128)} %get-tuple-element.5.table, f32[512,1,128]{2,1,0:T(1,128)} %get-tuple-element.6.table_e, f32[4,2,48,128]{3,2,1,0:T(8,128)} %get-tuple-element.7.blocks), custom_call_target="tpu_custom_call" | custom-call | tf_op jit(solution)/shard_map/finish/pallas_call | solution.py:490

commit v5 on v4

--- a/solution.py
+++ b/solution.py
@@ -131,7 +131,7 @@
 
 
 def sum_buckets(
-    counts, jac, res, cam, cam_map, part_b, part_g, part_e, inv, msg, hots, gothot, acc, ssem, rsem, hssem, hrsem, gots
+    counts, loads, jac, res, cam, cam_map, part_b, part_g, part_e, inv, msg, hots, gothot, acc, ssem, rsem, hssem, hrsem, gots
 ):
     chunk = 64 // len(gots)
     z, y, core, x = place()
@@ -147,6 +147,8 @@
     outside = [at(((z // 2) * 2 + i) % 8, y, core, x) for i in range(2, 8)]
     for peer in outside:
         pl.semaphore_signal(barrier, inc=1, device_id=peer, device_id_type=MESH)
+    for c in loads:
+        c.wait()
     lane = lax.broadcasted_iota(jnp.int32, (1, 128), 1)
 
     def pack(d, carry):
@@ -176,16 +178,25 @@
     )
     pl.semaphore_wait(barrier, 63 + len(outside))
 
-    def copy(i):
-        to = (me + i) % 64
-        return remote(msg.at[to], gots[(i - 1) // chunk].at[(i - 1) % chunk], ssem.at[i], rsem.at[i], device_of(to, z))
+    order = [(11 * k) % 64 for k in range(1, 64)]
+    window = 24
+
+    def copy(k):
+        to = (me + order[k]) % 64
+        return remote(msg.at[to], gots[k // chunk].at[k % chunk], ssem.at[k], rsem.at[k], device_of(to, z))
+
+    def push(c):
+        for k in range(c * chunk, min(c * chunk + chunk, 63)):
+            if k >= window:
+                copy(k - window).wait_send()
+            copy(k).start()
 
     def hot_copy(i):
         to = (me + i) % 64
         return remote(hots.at[to], gothot.at[i], hssem.at[i], hrsem.at[i], device_of(to, z))
 
-    for i in range(1, 64):
-        copy(i).start()
+    for c in range(window // chunk):
+        push(c)
     gots[-1][chunk - 1] = msg[me]
     acc[:, 4 * ROWS :] = jnp.zeros((HALF, 256 - 4 * ROWS), F32)
     acc[:, : 4 * ROWS] = weighted(ejac, eres, eids.astype(F32))
@@ -194,19 +205,24 @@
         hots[0:ROWS, q, :] = low[:, q * 128 : (q + 1) * 128]
         hots[0:ROWS, 4 + q, :] = high[:, q * 128 : (q + 1) * 128]
     hots[ROWS:64] = jnp.zeros((64 - ROWS, 8, 128), F32)
-    for i in range(1, 64):
-        hot_copy(i).start()
     gothot[0] = hots[me]
+    push(3)
     inv[...] = jnp.zeros_like(inv)
     inv[:, 0:16] = camera_ids_here(cam_map, hot)
     inv[0:1, 16:17] = jnp.full((1, 1), hot, jnp.int32)
+    push(4)
 
     acc[...] = jnp.zeros_like(acc)
     for c in range(64 // chunk):
-        for i in range(c * chunk + 1, min(c * chunk + chunk + 1, 64)):
-            copy(i).wait_recv()
+        for k in range(c * chunk, min(c * chunk + chunk, 63)):
+            copy(k).wait_recv()
         whole = jnp.concatenate([gots[c][s, h] for s in range(chunk) for h in range(2)], axis=1)
         acc[:, : 4 * ROWS] += weighted(whole[0:18], whole[18:20], whole[20:21])
+        if c < 3:
+            push(5 + c)
+        if c == 2:
+            for i in range(1, 64):
+                hot_copy(i).start()
     low, high = unfolded(acc)
     for i in range(1, 64):
         hot_copy(i).wait_recv()
@@ -222,8 +238,9 @@
             part_e[g, h, 1:2] = extra[g * 2 + h : g * 2 + h + 1]
 
     def finish():
+        for k in range(63 - window, 63):
+            copy(k).wait_send()
         for i in range(1, 64):
-            copy(i).wait_send()
             hot_copy(i).wait_send()
 
     return finish
@@ -236,7 +253,7 @@
         self.slots = slots_of(z, y, core, x)
         ys = [at(z, (y + i) % 4, core, x) for i in range(1, 4)]
         xs = [at(z, y, core, (x + i) % 4) for i in range(1, 4)]
-        self.zs = [at((z + i) % 8, y, core, x) for i in range(1, 8)]
+        self.zs = [at((z + i) % 8, y, core, x) for i in (4, 3, 5, 2, 6, 1, 7)]
         self.other = at(z, y, 1 - core, x)
         self.middle, self.last = (ys, xs), (xs, ys)
         self.mid, self.far = (y, x), (x, y)
@@ -270,21 +287,21 @@
         blocks = [self.slots[part] // 8 * 8 for part in range(2)]
         for part in range(2):
             self.wait_recv(part, 0, 7, 0, self.zs[0])
-            for i in range(3):
+            for i in (1, 0, 2):
                 self.start(part, blocks[part], 8, 1 + i, self.middle[part][i])
-            for i in range(3):
+            for i in (1, 0, 2):
                 self.start(part, blocks[part], 8, 4 + i, self.last[part][i])
             self.start(part, blocks[part], 8, 7, self.other)
         between[1]()
-        for i in range(3):
+        for i in (0, 2, 1):
             for part in range(2):
                 base = self.core * 128 + self.far[part] * 32 + (self.mid[part] + 3 - i) % 4 * 8
                 self.wait_recv(part, base, 8, 1 + i, self.middle[part][i])
-                for j in range(3):
+                for j in (1, 0, 2):
                     self.start(part, base, 8, 4 + j, self.last[part][j])
                 self.start(part, base, 8, 7, self.other)
         between[2]()
-        for j in range(3):
+        for j in (0, 2, 1):
             for part in range(2):
                 base = self.core * 128 + (self.far[part] + 3 - j) % 4 * 32
                 self.wait_recv(part, base, 32, 4 + j, self.last[part][j])
@@ -301,14 +318,19 @@
 
 
 def main_kernel(
-    counts, jac, res, cam, cam_map, table, table_e, blocks,
+    counts, jac_far, res_far, cam_far, map_far, table, table_e, blocks,
+    jac, res, cam, cam_map, lsem,
     part_b, part_g, part_e, found, inv, msg, hots, gothot, acc, ssem, rsem, hssem, hrsem, isem,
     got_b, got_g, got_e, mine_b, bx, bz, grad, grad_e,
     s2b, r2b, s2g, r2g, s2e, r2e, sx, rx, sz, rz, sg, rg, se, re, sg2, rg2, se2, re2,
     *gots,
 ):
+    far = ((jac_far, jac), (res_far, res), (cam_far, cam), (map_far, cam_map))
+    loads = [pltpu.make_async_copy(*pair, lsem.at[n]) for n, pair in enumerate(far)]
+    for c in loads:
+        c.start()
     sums_sent = sum_buckets(
-        counts, jac, res, cam, cam_map, part_b, part_g, part_e, found, msg, hots, gothot, acc, ssem, rsem, hssem, hrsem, gots
+        counts, loads, jac, res, cam, cam_map, part_b, part_g, part_e, found, msg, hots, gothot, acc, ssem, rsem, hssem, hrsem, gots
     )
     z, y, core, x = place()
     g, p = z // 2, z % 2
@@ -457,8 +479,13 @@
     table, table_e, blocks = call(
         main_kernel,
         (shape(2 * SLOTS, 8, 128), shape(2 * SLOTS, 1, 128), shape(4, 2, 48, 128)),
-        [SM(), VM(), VM(), VM(), VM()],
+        [SM()] + [pl.BlockSpec(memory_space=pl.ANY)] * 4,
         [
+            vmem(18, 32768),
+            vmem(2, 32768),
+            pltpu.VMEM((256, 128), jnp.int32),
+            pltpu.VMEM((512, 128), jnp.int32),
+            dma((4,)),
             vmem(4, 2, 48, 128),
             vmem(4, 2, 8, 128),
             vmem(4, 2, 2, 128),

time: 97.9 us -> 92.6 us (0.946)
  Pallas kernels: 97.1 us -> 91.8 us
    pallas_call x1, Pallas kernels: 92.8 us -> 87.5 us  [local(): call(main_kernel, (shape(2 * SLOTS, 8, 128), shape(2 * SLOTS, 1, 128), sh...]
where the time goes in v5:
time: 92.6 us; the launch traced here: 92.5 us
  Pallas kernels  91.8 us (99%)
    pallas_call x1, Pallas kernels, local(): call(main_kernel, (shape(2 * SLOTS, 8, 128), shape(2 * SLOTS, 1, 128), sh...  87.5 us
    pallas_call x1, Pallas kernels, local(): pl.pallas_call(finish_kernel, out_shape=(shape(9, 65536), shape(81, 1024)...  4.36 us

profile of v5, /device:TPU:1, one launch (start us, length us, event | category | flops | bytes accessed | tf_op | source)
XLA Modules:
  0.0 92.5 jit_solution(616338635896448327)
XLA Ops:
  0.6 87.5 %main.1 = (f32[512,8,128]{2,1,0:T(8,128)}, f32[512,1,128]{2,1,0:T(1,128)}, f32[4,2,48,128]{3,2,1,0:T(8,128)}) custom-call(s32[1,64]{1,0:T(1,128)} %counts.1, f32[18,32768]{1,0:T(8,128)} %jac_far.1, f32[2,32768]{1,0:T(2,128)} %res_far.1, s32[256,128]{1,0:T(8,128)} %bitcast.3, s32[512,128]{1,0:T(8,128)} %bitcast.2), custom_call_target="tpu_custom_call" | custom-call | tf_op jit(solution)/shard_map/main/pallas_call | solution.py:479
  88.1 4.4 %finish.1 = (f32[9,65536]{1,0:T(8,128)}, f32[81,1024]{1,0:T(8,128)}) custom-call(f32[512,8,128]{2,1,0:T(8,128)} %get-tuple-element.5.table, f32[512,1,128]{2,1,0:T(1,128)} %get-tuple-element.6.table_e, f32[4,2,48,128]{3,2,1,0:T(8,128)} %get-tuple-element.7.blocks), custom_call_target="tpu_custom_call" | custom-call | tf_op jit(solution)/shard_map/finish/pallas_call | solution.py:517

commit v6 on v5

--- a/solution.py
+++ b/solution.py
@@ -253,7 +253,8 @@
         self.slots = slots_of(z, y, core, x)
         ys = [at(z, (y + i) % 4, core, x) for i in range(1, 4)]
         xs = [at(z, y, core, (x + i) % 4) for i in range(1, 4)]
-        self.zs = [at((z + i) % 8, y, core, x) for i in (4, 3, 5, 2, 6, 1, 7)]
+        self.steps = (4, 3, 5, 2, 6, 1, 7)
+        self.zs = [at((z + i) % 8, y, core, x) for i in self.steps]
         self.other = at(z, y, 1 - core, x)
         self.middle, self.last = (ys, xs), (xs, ys)
         self.mid, self.far = (y, x), (x, y)
@@ -278,20 +279,26 @@
         for c in self.copies(*args):
             c.wait_recv()
 
+    def forward(self, part, slot):
+        for i in (1, 0, 2):
+            self.start(part, slot, 1, 1 + i, self.middle[part][i])
+        for i in (1, 0, 2):
+            self.start(part, slot, 1, 4 + i, self.last[part][i])
+        self.start(part, slot, 1, 7, self.other)
+
     def run(self, between=()):
         between = list(between) + [lambda: None] * 4
         for part in range(2):
-            for peer in self.zs:
-                self.start(part, self.slots[part], 1, 0, peer)
+            for n, peer in enumerate(self.zs):
+                self.start(part, self.slots[part], 1, 8 + n, peer)
+        for part in range(2):
+            self.forward(part, self.slots[part])
         between[0]()
-        blocks = [self.slots[part] // 8 * 8 for part in range(2)]
-        for part in range(2):
-            self.wait_recv(part, 0, 7, 0, self.zs[0])
-            for i in (1, 0, 2):
-                self.start(part, blocks[part], 8, 1 + i, self.middle[part][i])
-            for i in (1, 0, 2):
-                self.start(part, blocks[part], 8, 4 + i, self.last[part][i])
-            self.start(part, blocks[part], 8, 7, self.other)
+        for n in (6, 5, 4, 3, 2, 1, 0):
+            for part in range(2):
+                slot = self.slots[part] // 8 * 8 + (self.slots[part] + 8 - self.steps[n]) % 8
+                self.wait_recv(part, slot, 1, 8 + n, self.zs[n])
+                self.forward(part, slot)
         between[1]()
         for i in (0, 2, 1):
             for part in range(2):
@@ -312,7 +319,7 @@
 
     def finish(self):
         for part in range(2):
-            for sem, size in [(0, 7)] + [(k, 8) for k in (1, 2, 3)] + [(k, 32) for k in (4, 5, 6)] + [(7, 128)]:
+            for sem, size in [(8 + k, 1) for k in range(7)] + [(k, 8) for k in (1, 2, 3)] + [(k, 32) for k in (4, 5, 6)] + [(7, 128)]:
                 for c in self.copies(part, 0, size, sem, self.other):
                     c.wait_send()
 
@@ -403,16 +410,16 @@
 
         def pick(r, acc):
             top, low = acc
-            for k in range(16):
-                v = inv[h * 8 + r, k]
-                q = r * 16 + k
+            for k in range(64):
+                v = inv[h * 8 + r * 4 + k // 16, k % 16]
+                q = r * 64 + k
                 turn = (q - v) & 127
                 at_q = lane == q
                 top = jnp.where(at_q, pltpu.roll(grad[v >> 7], turn, 1), top)
                 low = jnp.where(at_q, pltpu.roll(grad_e[v >> 7], turn, 1), low)
             return top, low
 
-        top, low = lax.fori_loop(0, 8, pick, (jnp.zeros((8, 128), F32), jnp.zeros((2, 128), F32)))
+        top, low = lax.fori_loop(0, 2, pick, (jnp.zeros((8, 128), F32), jnp.zeros((2, 128), F32)))
         table[h * SLOTS + second.slots[h]] = top
         table_e[h * SLOTS + second.slots[h]] = low[0:1]
 
@@ -509,7 +516,7 @@
             vmem(2 * SLOTS + 8, 2, 128),
         ]
         + [dma((3,))] * 10
-        + [dma((2, 8))] * 8
+        + [dma((2, 16))] * 8
         + [vmem(8, 2, MSG, 128)] * 8,
         cid=1,
         name="main",

time: 92.6 us -> 92.3 us (level)
  no operation moved by 1% of the time
where the time goes in v6:
time: 92.3 us; the launch traced here: 92.1 us
  Pallas kernels  91.5 us (99%)
    pallas_call x1, Pallas kernels, local(): call(main_kernel, (shape(2 * SLOTS, 8, 128), shape(2 * SLOTS, 1, 128), sh...  87.1 us
    pallas_call x1, Pallas kernels, local(): pl.pallas_call(finish_kernel, out_shape=(shape(9, 65536), shape(81, 1024)...  4.36 us

profile of v6, /device:TPU:1, one launch (start us, length us, event | category | flops | bytes accessed | tf_op | source)
XLA Modules:
  0.0 92.1 jit_solution(18130840935597516326)
XLA Ops:
  0.6 87.1 %main.1 = (f32[512,8,128]{2,1,0:T(8,128)}, f32[512,1,128]{2,1,0:T(1,128)}, f32[4,2,48,128]{3,2,1,0:T(8,128)}) custom-call(s32[1,64]{1,0:T(1,128)} %counts.1, f32[18,32768]{1,0:T(8,128)} %jac_far.1, f32[2,32768]{1,0:T(2,128)} %res_far.1, s32[256,128]{1,0:T(8,128)} %bitcast.3, s32[512,128]{1,0:T(8,128)} %bitcast.2), custom_call_target="tpu_custom_call" | custom-call | tf_op jit(solution)/shard_map/main/pallas_call | solution.py:486
  87.8 4.4 %finish.1 = (f32[9,65536]{1,0:T(8,128)}, f32[81,1024]{1,0:T(8,128)}) custom-call(f32[512,8,128]{2,1,0:T(8,128)} %get-tuple-element.5.table, f32[512,1,128]{2,1,0:T(1,128)} %get-tuple-element.6.table_e, f32[4,2,48,128]{3,2,1,0:T(8,128)} %get-tuple-element.7.blocks), custom_call_target="tpu_custom_call" | custom-call | tf_op jit(solution)/shard_map/finish/pallas_call | solution.py:524

commit v7 on v5

--- a/solution.py
+++ b/solution.py
@@ -226,7 +226,7 @@
     low, high = unfolded(acc)
     for i in range(1, 64):
         hot_copy(i).wait_recv()
-    extra = lax.fori_loop(0, 64, lambda s, t: t + gothot[s], jnp.zeros((8, 128), F32))
+    extra = jnp.sum(gothot[...], axis=0)
     for g in range(4):
         part = low if g < 2 else high
         for h in range(2):
@@ -403,16 +403,16 @@
 
         def pick(r, acc):
             top, low = acc
-            for k in range(16):
-                v = inv[h * 8 + r, k]
-                q = r * 16 + k
+            for k in range(64):
+                v = inv[h * 8 + r * 4 + k // 16, k % 16]
+                q = r * 64 + k
                 turn = (q - v) & 127
                 at_q = lane == q
                 top = jnp.where(at_q, pltpu.roll(grad[v >> 7], turn, 1), top)
                 low = jnp.where(at_q, pltpu.roll(grad_e[v >> 7], turn, 1), low)
             return top, low
 
-        top, low = lax.fori_loop(0, 8, pick, (jnp.zeros((8, 128), F32), jnp.zeros((2, 128), F32)))
+        top, low = lax.fori_loop(0, 2, pick, (jnp.zeros((8, 128), F32), jnp.zeros((2, 128), F32)))
         table[h * SLOTS + second.slots[h]] = top
         table_e[h * SLOTS + second.slots[h]] = low[0:1]
 
@@ -438,16 +438,14 @@
     for n in range(table.shape[0]):
         out[0:8, n * 128 : (n + 1) * 128] = table[n]
         out[8:9, n * 128 : (n + 1) * 128] = table_e[n]
-    for h in range(2):
-        whole = blocks[0, h]
-        here = slice(h * 128, (h + 1) * 128)
-        for k in range(9):
-            for j in range(5):
-                m = (k + j) % 9
-                t = 40 + j if k == 8 else j * 8 + k
-                blocks_out[k * 9 + m : k * 9 + m + 1, here] = whole[t : t + 1]
-                if j:
-                    blocks_out[m * 9 + k : m * 9 + k + 1, here] = whole[t : t + 1]
+    whole = blocks[0, 0]
+    for k in range(9):
+        for j in range(5):
+            m = (k + j) % 9
+            t = 40 + j if k == 8 else j * 8 + k
+            blocks_out[k * 9 + m : k * 9 + m + 1, :] = whole[t : t + 1]
+            if j:
+                blocks_out[m * 9 + k : m * 9 + k + 1, :] = whole[t : t + 1]
 
 
 def shape(*dims, dtype=F32):
@@ -517,13 +515,13 @@
     return pl.pallas_call(
         finish_kernel,
         out_shape=(shape(9, 65536), shape(81, 1024)),
-        grid=(4,),
+        grid=(8,),
         in_specs=[
-            pl.BlockSpec((2 * SLOTS // 4, 8, 128), lambda n: (n, 0, 0)),
-            pl.BlockSpec((2 * SLOTS // 4, 1, 128), lambda n: (n, 0, 0)),
-            pl.BlockSpec((1, 2, 48, 128), lambda n: (n, 0, 0, 0)),
+            pl.BlockSpec((2 * SLOTS // 8, 8, 128), lambda n: (n, 0, 0)),
+            pl.BlockSpec((2 * SLOTS // 8, 1, 128), lambda n: (n, 0, 0)),
+            pl.BlockSpec((1, 1, 48, 128), lambda n: (n // 2, n % 2, 0, 0)),
         ],
-        out_specs=(pl.BlockSpec((9, 16384), lambda n: (0, n)), pl.BlockSpec((81, 256), lambda n: (0, n))),
+        out_specs=(pl.BlockSpec((9, 8192), lambda n: (0, n)), pl.BlockSpec((81, 128), lambda n: (0, n))),
         name="finish",
     )(table, table_e, blocks)
 

time: 92.6 us -> 93.5 us (level)
    pallas_call x1, Pallas kernels: 4.36 us -> 6.26 us  [local(): pl.pallas_call(finish_kernel, out_shape=(shape(9, 65536), shape(81, 1024)...]
    pallas_call x1, Pallas kernels: 87.5 us -> 86.4 us  [local(): call(main_kernel, (shape(2 * SLOTS, 8, 128), shape(2 * SLOTS, 1, 128), sh...]
where the time goes in v7:
time: 93.5 us; the launch traced here: 93.3 us
  Pallas kernels  92.6 us (99%)
    pallas_call x1, Pallas kernels, local(): call(main_kernel, (shape(2 * SLOTS, 8, 128), shape(2 * SLOTS, 1, 128), sh...  86.4 us
    pallas_call x1, Pallas kernels, local(): pl.pallas_call(finish_kernel, out_shape=(shape(9, 65536), shape(81, 1024)...  6.26 us

profile of v7, /device:TPU:1, one launch (start us, length us, event | category | flops | bytes accessed | tf_op | source)
XLA Modules:
  0.0 93.3 jit_solution(1822744937304515148)
XLA Ops:
  0.6 86.4 %main.1 = (f32[512,8,128]{2,1,0:T(8,128)}, f32[512,1,128]{2,1,0:T(1,128)}, f32[4,2,48,128]{3,2,1,0:T(8,128)}) custom-call(s32[1,64]{1,0:T(1,128)} %counts.1, f32[18,32768]{1,0:T(8,128)} %jac_far.1, f32[2,32768]{1,0:T(2,128)} %res_far.1, s32[256,128]{1,0:T(8,128)} %bitcast.3, s32[512,128]{1,0:T(8,128)} %bitcast.2), custom_call_target="tpu_custom_call" | custom-call | tf_op jit(solution)/shard_map/main/pallas_call | solution.py:477
  87.0 6.3 %finish.1 = (f32[9,65536]{1,0:T(8,128)}, f32[81,1024]{1,0:T(8,128)}) custom-call(f32[512,8,128]{2,1,0:T(8,128)} %get-tuple-element.5.table, f32[512,1,128]{2,1,0:T(1,128)} %get-tuple-element.6.table_e, f32[4,2,48,128]{3,2,1,0:T(8,128)} %get-tuple-element.7.blocks), custom_call_target="tpu_custom_call" | custom-call | tf_op jit(solution)/shard_map/finish/pallas_call | solution.py:515
